TPU v7x, 32 devices: a whole 2x2x4 slice. The times are simulated.
32 devices in a mesh: expert: 4 (over y, x), tensor: 4 (over z), rep: 2 (over core).
Axes of the slice: x: 2, y: 2, z: 4, core: 2. Of those that a mesh axis runs over, the one named last changes fastest.
Arguments:
- requests: bfloat16 [512, 1536], P('expert', ('tensor', 'rep')), may hold values from -6 to 6
- expert_ids: int32 [512, 2], P('expert'), may hold values from 0 to 3, all different within a row; in each aligned block of 128 rows (0 to 127, 128 to 255, ...) at most 96 rows name the same one
- gate_values: float32 [512, 2], P('expert'), may hold values from 0.2 to 1
- w_up: bfloat16 [4, 1536, 6144], P(None, 'expert', ('tensor', 'rep')), may hold values from -0.15625 to 0.15625
- w_down: bfloat16 [4, 1536, 6144], P(None, 'expert', ('tensor', 'rep')), may hold values from -0.078125 to 0.078125
- tower_in: bfloat16 [1536, 768], P(('tensor', 'rep')), may hold values from -0.15625 to 0.15625
- tower_bias: float32 [768], replicated, may hold values from -3 to 3
- tower_out: float32 [3, 256], replicated, may hold values from -0.375 to 0.375
- out_bias: float32 [3], replicated, may hold values from -3 to 3
Outputs:
- mixed: bfloat16 [512, 1536], P('expert', ('tensor', 'rep'))
- scores: float32 [3, 512], P(None, ('expert', 'tensor', 'rep'))
Inputs may be any that keep to these rules, and one draw needn't show every extreme that they name: `expert_ids`: each row names two different experts. In the rows of one device (128 requests) no expert is named more than 96 times, a bound that some block reaches.
All inputs are finite; a program needn't handle non-finite values.
Results may differ from a plain program's by a relative error of at most 0.015.
Values may be sent and summed in bfloat16 or wider, within the bound.
A program may use at most 64 MiB of HBM per device.

v0:
```python
import functools
import jax
import jax.numpy as jnp
from jax import lax
from jax.experimental import pallas as pl
from jax.experimental.pallas import tpu as pltpu
from jax.sharding import PartitionSpec as P

MESH = pl.DeviceIdType.MESH
CHUNKS = 4
F32 = jnp.float32
BF16 = jnp.bfloat16


def stay_kernel(
    dims, req_hbm, ids_hbm, gates_hbm, up_hbm, down_hbm, tin_hbm, bias_hbm, tout_hbm, ob_ref,
    mixed_ref, scores_ref,
    req_ref, ids_ref, gates_ref, bias_ref, tout_ref, up, down, tin, ag, meta_ref, meta, xin, xs, hp, r1, s2, r2, hid, mine, dsend0, drecv0, dsend, drecv,
    fsend, frecv, mixed_rows, lsem, ag_s, ag_r, me_s, me_r, x_s, x_r, s1_s, s1_r, s2_s, s2_r, h_s, h_r,
    p_s, p_r, d_s, d_r, f_s, f_r,
):
    nx, nt, nr, experts, tok, feat, hcols, tasks, th = dims
    xe, t, r = lax.axis_index("expert"), lax.axis_index("tensor"), lax.axis_index("rep")
    sub = tok // CHUNKS
    started = []

    def remote(src, dst, ssem, rsem, dev):
        return pltpu.make_async_remote_copy(
            src_ref=src, dst_ref=dst, send_sem=ssem, recv_sem=rsem, device_id=dev,
            device_id_type=MESH)

    def send(src, dst, ssem, rsem, dev):
        copy = remote(src, dst, ssem, rsem, dev)
        copy.start()
        started.append((None, copy))

    def send_if(cond, src, dst, ssem, rsem, dev):
        copy = remote(src, dst, ssem, rsem, dev)

        @pl.when(cond)
        def _():
            copy.start()
        started.append((cond, copy))

    def got(ref, ssem, rsem):
        remote(ref, ref, ssem, rsem, (xe, t, r)).wait_recv()

    first = [
        pltpu.make_async_copy(req_hbm, req_ref, lsem.at[3]),
        pltpu.make_async_copy(ids_hbm, ids_ref, lsem.at[4]),
        pltpu.make_async_copy(gates_hbm, gates_ref, lsem.at[5]),
    ]
    loads = [
        pltpu.make_async_copy(up_hbm, up, lsem.at[0]),
        pltpu.make_async_copy(down_hbm, down, lsem.at[1]),
        pltpu.make_async_copy(tin_hbm, tin, lsem.at[2]),
        pltpu.make_async_copy(bias_hbm, bias_ref, lsem.at[6]),
        pltpu.make_async_copy(tout_hbm, tout_ref, lsem.at[7]),
    ]
    for load in first + loads:
        load.start()
    here = t == xe
    barrier = pltpu.get_barrier_semaphore()

    def greet(dev):
        pl.semaphore_signal(barrier, inc=1, device_id=dev, device_id_type=MESH)

    me = t * nr + r
    for d in range(1, nt * nr):
        other = me ^ d
        greet((xe, lax.div(other, nr), lax.rem(other, nr)))
    for d in range(1, nx):
        for flip in range(nr):
            greet((xe ^ d, t, r ^ flip))
    for b in range(nx):
        @pl.when(jnp.logical_not(jnp.logical_and(here, xe == b)))
        def _():
            greet((b, xe, r))

        @pl.when(jnp.logical_not(jnp.logical_and(here, t == b)))
        def _():
            greet((t, b, r))
    for load in first:
        load.wait()
    meta_ref[...] = jnp.concatenate(
        [ids_ref[...].astype(F32), gates_ref[...], jnp.zeros((4, tok), F32)], axis=0)
    greeted = (nt * nr - 1) + (nx - 1) * nr + 2 * nx

    @pl.when(here)
    def _():
        pl.semaphore_wait(barrier, greeted - 2)

    @pl.when(jnp.logical_not(here))
    def _():
        pl.semaphore_wait(barrier, greeted)

    for d in range(1, nt):
        to = lax.rem(t + d, nt)
        send(req_ref, ag.at[t], ag_s.at[d], ag_r.at[t], (xe, to, r))
    for d in range(1, nx):
        send(meta_ref, meta.at[xe], me_s.at[d], me_r.at[xe], (xe ^ d, t, r))
    meta[xe] = meta_ref[...]

    for d in (3, 1, 2, 0):
        tx = xe ^ d
        own = tx == t

        @pl.when(jnp.logical_not(own))
        def _():
            got(ag.at[tx], ag_s.at[0], ag_r.at[tx])
        for flip in (0, 1):
            if d == 0 and flip == 0:
                continue
            ss, rs = x_s.at[2 * d + flip], x_r.at[xe, r]
            dev = (tx, t, r ^ flip)
            send_if(own, req_ref, xin.at[xe, r], ss, rs, dev)
            send_if(jnp.logical_not(own), ag.at[tx], xin.at[xe, r], ss, rs, dev)

    is_own = xe == t

    @pl.when(is_own)
    def _():
        xin[xe, r] = req_ref[...]

    @pl.when(jnp.logical_not(is_own))
    def _():
        xin[xe, r] = ag[xe]

    for d in range(1, nx):
        got(meta.at[xe ^ d], me_s.at[0], me_r.at[xe ^ d])
    for d in range(nx):
        for flip in range(nr):
            if d == 0 and flip == 0:
                continue
            slot = (xe ^ d, r ^ flip)
            got(xin.at[slot], x_s.at[0], x_r.at[slot])
    for b in range(nx):
        for k in range(nr):
            xs[b, :, k * feat:(k + 1) * feat] = xin[b, k].T
    info = [meta[b].T for b in range(nx)]

    def column(c, j):
        return jnp.concatenate([info[b][c * sub:(c + 1) * sub, j:j + 1] for b in range(nx)], axis=0)

    loads[0].wait()
    quarter = xe
    near = (1, 2)
    def up_chunk(c):
        rows = xs[:, c * sub:(c + 1) * sub, :].reshape(nx * sub, nr * feat)
        ids = (column(c, 0), column(c, 1))
        for h in range(2):
            picked = [jnp.zeros((nx * sub, hcols), F32)] * 2
            for e in range(experts):
                part = jnp.dot(rows, up[e, :, h * hcols:(h + 1) * hcols], preferred_element_type=F32)
                picked = [jnp.where(ids[k] == float(e), part, picked[k]) for k in range(2)]
            for k in range(2):
                hp[c, h, :, k * sub:(k + 1) * sub, :] = picked[k].astype(BF16).reshape(nx, sub, hcols)
            fa, fb = near[h], near[1 - h]
            for i, q in enumerate((quarter ^ fa ^ fb, quarter ^ fa)):
                send(hp.at[c, h, q], r1.at[c, h, i], s1_s.at[c, h, i], s1_r.at[c, h, i],
                     (xe ^ fa, t, r))

    def reduce_first(c, h):
        fa, fb = near[h], near[1 - h]
        got(r1.at[c, h, 0], s1_s.at[c, h, 0], s1_r.at[c, h, 0])
        s2[c, h] = (hp[c, h, quarter ^ fb].astype(F32) + r1[c, h, 0].astype(F32)).astype(BF16)
        send(s2.at[c, h], r2.at[c, h], s2_s.at[c, h], s2_r.at[c, h], (xe ^ fb, t, r))

    def reduce_second(c, h):
        fa, fb = near[h], near[1 - h]
        got(r1.at[c, h, 1], s1_s.at[c, h, 1], s1_r.at[c, h, 1])
        got(r2.at[c, h], s2_s.at[c, h], s2_r.at[c, h])
        total = (hp[c, h, quarter].astype(F32) + r1[c, h, 1].astype(F32)) + r2[c, h].astype(F32)
        hid[c, h, quarter] = jnp.maximum(total, 0.0).astype(BF16)
        for i, f in enumerate((fb, fa)):
            send(hid.at[c, h, quarter], hid.at[c, h, quarter], h_s.at[c, h, i],
                 h_r.at[c, h, quarter], (xe ^ f, t, r))

    def forward(c, h):
        fa, fb = near[h], near[1 - h]
        q = quarter ^ fb
        got(hid.at[c, h, q], h_s.at[c, h, 2], h_r.at[c, h, q])
        send(hid.at[c, h, q], hid.at[c, h, q], h_s.at[c, h, 2], h_r.at[c, h, q], (xe ^ fa, t, r))

    def collect(c, h):
        fa, fb = near[h], near[1 - h]
        for q in (quarter ^ fa, quarter ^ fa ^ fb):
            got(hid.at[c, h, q], h_s.at[c, h, 2], h_r.at[c, h, q])

    def down_chunk(c):
        ids = (column(c, 0), column(c, 1))
        gates = (column(c, 2), column(c, 3))
        total = jnp.zeros((nx * sub, nr * feat), F32)
        for e in range(experts):
            hit = (ids[0] == float(e), ids[1] == float(e))
            weight = jnp.where(hit[0], gates[0], 0.0) + jnp.where(hit[1], gates[1], 0.0)
            part = None
            for h in range(2):
                values = [hid[c, h, :, k * sub:(k + 1) * sub, :].reshape(nx * sub, hcols)
                          for k in range(2)]
                chosen = jnp.where(hit[0], values[0], jnp.where(hit[1], values[1], jnp.zeros_like(values[1])))
                one = lax.dot_general(chosen, down[e, :, h * hcols:(h + 1) * hcols],
                                      (((1,), (1,)), ((), ())), preferred_element_type=F32)
                part = one if part is None else part + one
            total = total + weight * part
        low, high = total[:, :feat], total[:, feat:]
        mine[c] = jnp.where(r == 0, low, high).reshape(nx, sub, feat)
        dsend0[c] = jnp.where(r == 0, high, low).astype(BF16).reshape(nx, sub, feat)
        send(dsend0.at[c], drecv0.at[c], p_s.at[c], p_r.at[c], (xe, t, 1 - r))

    def pair_chunk(c):
        got(drecv0.at[c], p_s.at[c], p_r.at[c])
        dsend[c] = (mine[c] + drecv0[c].astype(F32)).astype(BF16)
        for b in range(nx):
            self_copy = jnp.logical_and(here, xe == b)

            @pl.when(self_copy)
            def _():
                drecv[c, t] = dsend[c, b]
            send_if(jnp.logical_not(self_copy), dsend.at[c, b], drecv.at[c, t], d_s.at[c, b],
                    d_r.at[c, t], (b, xe, r))

    def mixed_chunk(c):
        for src in range(nt):
            @pl.when(jnp.logical_not(jnp.logical_and(here, t == src)))
            def _():
                got(drecv.at[c, src], d_s.at[c, 0], d_r.at[c, src])
        total = drecv[c, 0].astype(F32)
        for src in range(1, nt):
            total = total + drecv[c, src].astype(F32)
        value = total.astype(BF16)
        mixed_rows[c * sub:(c + 1) * sub, :] = value
        part = jnp.dot(value, tin[...], preferred_element_type=F32).astype(BF16)
        each = tok // (nt * nr)
        per = sub // each
        fsend[c * per:(c + 1) * per] = part.reshape(per, each, part.shape[1])
        for to in range(c * per, (c + 1) * per):
            send_if(me != to, fsend.at[to], frecv.at[me], f_s.at[to], f_r.at[me],
                    (xe, to // nr, to % nr))

    def both(stage, c):
        if 0 <= c < CHUNKS:
            for h in range(2):
                stage(c, h)

    def one(stage, c):
        if 0 <= c < CHUNKS:
            stage(c)

    for i in range(CHUNKS + 6):
        if i == 5:
            for load in loads[1:]:
                load.wait()
        both(forward, i - 4)
        both(reduce_second, i - 3)
        both(reduce_first, i - 2)
        one(up_chunk, i)
        both(collect, i - 5)
        one(down_chunk, i - 5)
        one(pair_chunk, i - 6)
    for c in range(CHUNKS):
        mixed_chunk(c)
    mixed_ref[...] = mixed_rows[...].T
    pre = fsend[me].astype(F32)
    for d in range(1, nt * nr):
        frm = me ^ d
        got(frecv.at[frm], f_s.at[0], f_r.at[frm])
        pre = pre + frecv[frm].astype(F32)
    active = jnp.maximum(pre + bias_ref[...].reshape(1, tasks * th), 0.0)
    outs = []
    for j in range(tasks):
        outs.append(jnp.sum(active[:, j * th:(j + 1) * th] * tout_ref[j:j + 1, :], axis=1, keepdims=True))
    each = pre.shape[0]
    lane = lax.broadcasted_iota(jnp.int32, (each, 128), 1)
    logits = jnp.zeros((each, 128), F32)
    for j in range(tasks):
        logits = jnp.where(lane == j, outs[j] + ob_ref[j], logits)
    scores_ref[...] = jax.nn.sigmoid(logits.T[:tasks, :])
    for cond, copy in started:
        if cond is None:
            copy.wait_send()
        else:
            @pl.when(cond)
            def _(copy=copy):
                copy.wait_send()


def stay_device(requests, expert_ids, gate_values, w_up, w_down, tower_in, tower_bias, tower_out,
                out_bias):
    nx, nt, nr = lax.axis_size("expert"), lax.axis_size("tensor"), lax.axis_size("rep")
    experts, _, hid_cols = w_up.shape
    tok, feat = requests.shape
    tasks, th = tower_out.shape
    hcols = hid_cols // 2
    sub = tok // CHUNKS
    each = tok // (nt * nr)
    dims = (nx, nt, nr, experts, tok, feat, hcols, tasks, th)
    vmem = pl.BlockSpec(memory_space=pltpu.VMEM)
    hbm = pl.BlockSpec(memory_space=pltpu.HBM)
    smem = pl.BlockSpec(memory_space=pltpu.SMEM)
    dma = pltpu.SemaphoreType.DMA
    C = CHUNKS
    scratch = [
        pltpu.VMEM((feat, tok), BF16), pltpu.VMEM((2, tok), jnp.int32), pltpu.VMEM((2, tok), F32),
        pltpu.VMEM(tower_bias.shape, F32), pltpu.VMEM(tower_out.shape, F32),
        pltpu.VMEM(w_up.shape, BF16), pltpu.VMEM(w_down.shape, BF16),
        pltpu.VMEM(tower_in.shape, BF16),
        pltpu.VMEM((nt, feat, tok), BF16), pltpu.VMEM((8, tok), F32), pltpu.VMEM((nx, 8, tok), F32),
        pltpu.VMEM((nx, nr, feat, tok), BF16), pltpu.VMEM((nx, tok, nr * feat), BF16),
        pltpu.VMEM((C, 2, nx, 2 * sub, hcols), BF16),
        pltpu.VMEM((C, 2, 2, 2 * sub, hcols), BF16),
        pltpu.VMEM((C, 2, 2 * sub, hcols), BF16), pltpu.VMEM((C, 2, 2 * sub, hcols), BF16),
        pltpu.VMEM((C, 2, nx, 2 * sub, hcols), BF16),
        pltpu.VMEM((C, nx, sub, feat), F32), pltpu.VMEM((C, nx, sub, feat), BF16),
        pltpu.VMEM((C, nx, sub, feat), BF16), pltpu.VMEM((C, nx, sub, feat), BF16),
        pltpu.VMEM((C, nt, sub, feat), BF16),
        pltpu.VMEM((nt * nr, each, tasks * th), BF16), pltpu.VMEM((nt * nr, each, tasks * th), BF16),
        pltpu.VMEM((tok, feat), BF16),
        dma((8,)), dma((nt,)), dma((nt,)), dma((nx,)), dma((nx,)), dma((2 * nx,)), dma((nx, nr)),
        dma((C, 2, 2)), dma((C, 2, 2)), dma((C, 2)), dma((C, 2)), dma((C, 2, 3)), dma((C, 2, nx)),
        dma((C,)), dma((C,)), dma((C, nx)), dma((C, nt)), dma((nt * nr,)), dma((nt * nr,)),
    ]
    mixed, scores = pl.pallas_call(
        functools.partial(stay_kernel, dims),
        out_shape=(jax.ShapeDtypeStruct((feat, tok), BF16), jax.ShapeDtypeStruct((tasks, each), F32)),
        in_specs=[hbm] * 8 + [smem],
        out_specs=(vmem, vmem),
        scratch_shapes=scratch,
        compiler_params=pltpu.CompilerParams(
            has_side_effects=True, collective_id=0, vmem_limit_bytes=60 << 20),
        name="stay",
    )(requests.T, expert_ids.T, gate_values.T, w_up, w_down, tower_in, tower_bias, tower_out, out_bias)
    return mixed.T, scores


def weights_stay(mesh):
    return mesh.shape["expert"] == 4 and mesh.shape["tensor"] == 4 and mesh.shape["rep"] == 2


def tower_head(pre, tower_bias, tower_out, out_bias):
    active = jax.nn.relu(pre + tower_bias[None, :])
    active = active.reshape(pre.shape[0], tower_out.shape[0], tower_out.shape[1])
    logits = jnp.sum(active * tower_out[None, :, :], axis=2) + out_bias[None, :]
    return jax.nn.sigmoid(logits).T


def per_device(
    requests, expert_ids, gate_values, w_up, w_down, tower_in, tower_bias, tower_out, out_bias
):
    groups = lax.axis_size("expert")
    experts = w_up.shape[0]
    local_experts = experts // groups
    tok_rows = requests.shape[0]
    capacity = 3 * tok_rows // experts
    serve_up, serve_down = (
        lax.all_to_all(w_up, "expert", split_axis=0, concat_axis=1, tiled=True),
        lax.all_to_all(w_down, "expert", split_axis=0, concat_axis=1, tiled=True),
    )
    flat_ids = expert_ids.reshape(-1)
    onehot = (flat_ids[:, None] == jnp.arange(experts, dtype=jnp.int32)[None, :]).astype(jnp.int32)
    before = jnp.cumsum(onehot, axis=0) - onehot
    slot_rank = jnp.sum(before * onehot, axis=1)
    slots = (flat_ids * capacity + slot_rank).reshape(tok_rows, 2)
    slot_index = jnp.arange(experts * capacity, dtype=jnp.int32)
    spread = (
        (slot_index[:, None] == slots[None, :, 0]) | (slot_index[:, None] == slots[None, :, 1])
    ).astype(jnp.bfloat16)
    full_rows = lax.all_gather(requests, ("tensor", "rep"), axis=1, tiled=True)
    outgoing = jnp.dot(spread, full_rows, preferred_element_type=jnp.float32).astype(jnp.bfloat16)
    incoming = lax.all_to_all(outgoing, "expert", split_axis=0, concat_axis=0, tiled=True)
    shaped = incoming.reshape(groups, local_experts, capacity, incoming.shape[1])
    hidden_pre = jnp.einsum("secd,edh->sech", shaped, serve_up, preferred_element_type=jnp.float32)
    hidden = jax.nn.relu(hidden_pre).astype(jnp.bfloat16)
    partial_value = jnp.einsum(
        "sech,edh->secd", hidden, serve_down, preferred_element_type=jnp.float32
    )
    summed = lax.psum_scatter(
        partial_value.astype(jnp.bfloat16), ("tensor", "rep"), scatter_dimension=3, tiled=True
    ).astype(jnp.float32)
    expert_out = summed.astype(jnp.bfloat16).reshape(
        groups * local_experts * capacity, summed.shape[3]
    )
    returned = lax.all_to_all(expert_out, "expert", split_axis=0, concat_axis=0, tiled=True)
    pick_first = (slots[:, 0:1] == slot_index[None, :]).astype(jnp.bfloat16)
    pick_second = (slots[:, 1:2] == slot_index[None, :]).astype(jnp.bfloat16)
    first = jnp.dot(pick_first, returned, preferred_element_type=jnp.float32)
    second = jnp.dot(pick_second, returned, preferred_element_type=jnp.float32)
    mixed = (gate_values[:, 0:1] * first + gate_values[:, 1:2] * second).astype(jnp.bfloat16)
    pre = lax.psum_scatter(
        jnp.dot(mixed, tower_in, preferred_element_type=jnp.float32).astype(jnp.bfloat16),
        ("tensor", "rep"),
        scatter_dimension=0,
        tiled=True,
    ).astype(jnp.float32)
    scores = tower_head(pre, tower_bias, tower_out, out_bias)
    return (mixed, scores)


def solution(mesh):
    in_specs = (
        P("expert", ("tensor", "rep")),
        P("expert", None),
        P("expert", None),
        P(None, "expert", ("tensor", "rep")),
        P(None, "expert", ("tensor", "rep")),
        P(("tensor", "rep"), None),
        P(),
        P(),
        P(),
    )
    out_specs = (P("expert", ("tensor", "rep")), P(None, ("expert", "tensor", "rep")))
    body = stay_device if weights_stay(mesh) else per_device
    return jax.shard_map(
        body, mesh=mesh, in_specs=in_specs, out_specs=out_specs, check_vma=False
    )
```

profile of v0, /device:TPU:25, one launch (start us, length us, event | category | flops | bytes accessed | tf_op | source)
XLA Modules:
  0.0 70.0 jit_solution(3480627901457347521)
XLA Ops:
  0.6 66.7 %stay.1 = (bf16[192,128]{1,0:T(8,128)(2,1)}, f32[3,16]{1,0:T(4,128)}) custom-call(bf16[192,128]{1,0:T(8,128)(2,1)} %bitcast.4, s32[2,128]{1,0:T(2,128)} %bitcast.6, f32[2,128]{1,0:T(2,128)} %bitcast.7, bf16[4,384,768]{2,1,0:T(8,128)(2,1)} %up_hbm.1, bf16[4,384,768]{2,1,0:T(8,128)(2,1)} %down_hbm.1, bf16[192,768]{1,0:T(8,128)(2,1)} %tin_hbm.1, f32[768]{0:T(1024)} %bias_hbm.1, ...), custom_call_target="tpu_custom_call" | custom-call | tf_op jit(solution)/shard_map/stay/pallas_call | solution.py:323
  67.4 1.4 %copy.13 = bf16[128,192]{0,1:T(8,128)(2,1)} copy(bf16[128,192]{0,1:T(8,128)(2,1)} %bitcast.5) | data formatting | bytes 98304
  68.8 1.2 %copy.14 = f32[3,16]{1,0:T(4,128)} copy(f32[3,16]{1,0:T(4,128)} %get-tuple-element.9) | data formatting | bytes 384
where the time goes:
time: 71.1 us; the launch traced here: 70 us
  Pallas kernels  66.7 us (94%)
  local copies, waits for them, and re-layouts  2.66 us (4%)
    pallas_call x1, Pallas kernels, stay_device(): pl.pallas_call(functools.partial(stay_kernel, dims), out_shape=(jax.Shape...  66.7 us
    unnamed x2, local copies, waits for them, and re-layouts  2.66 us

commit v1 on v0

--- a/solution.py
+++ b/solution.py
@@ -15,9 +15,9 @@
 def stay_kernel(
     dims, req_hbm, ids_hbm, gates_hbm, up_hbm, down_hbm, tin_hbm, bias_hbm, tout_hbm, ob_ref,
     mixed_ref, scores_ref,
-    req_ref, ids_ref, gates_ref, bias_ref, tout_ref, up, down, tin, ag, meta_ref, meta, xin, xs, hp, r1, s2, r2, hid, mine, dsend0, drecv0, dsend, drecv,
-    fsend, frecv, mixed_rows, lsem, ag_s, ag_r, me_s, me_r, x_s, x_r, s1_s, s1_r, s2_s, s2_r, h_s, h_r,
-    p_s, p_r, d_s, d_r, f_s, f_r,
+    req_ref, ids_ref, gates_ref, bias_ref, tout_ref, up, down, tin, meta_ref, meta, xin, xs, hp, r1, s2, r2, hid, mine, dsend0, drecv0, dsend, gat, zrec,
+    fsend, frecv, mixed_rows, lsem, me_s, me_r, x_s, x_r, q_s, q_r, s1_s, s1_r, s2_s, s2_r, h_s, h_r,
+    p_s, p_r, g_s, g_r, z_s, z_r, f_s, f_r,
 ):
     nx, nt, nr, experts, tok, feat, hcols, tasks, th = dims
     xe, t, r = lax.axis_index("expert"), lax.axis_index("tensor"), lax.axis_index("rep")
@@ -41,6 +41,16 @@
         def _():
             copy.start()
         started.append((cond, copy))
+
+    def drain():
+        for cond, copy in started:
+            if cond is None:
+                copy.wait_send()
+            else:
+                @pl.when(cond)
+                def _(copy=copy):
+                    copy.wait_send()
+        started.clear()
 
     def got(ref, ssem, rsem):
         remote(ref, ref, ssem, rsem, (xe, t, r)).wait_recv()
@@ -60,6 +70,8 @@
     for load in first + loads:
         load.start()
     here = t == xe
+    away = jnp.logical_not(here)
+    partner = (xe, t, 1 - r)
     barrier = pltpu.get_barrier_semaphore()
 
     def greet(dev):
@@ -70,74 +82,60 @@
         other = me ^ d
         greet((xe, lax.div(other, nr), lax.rem(other, nr)))
     for d in range(1, nx):
-        for flip in range(nr):
-            greet((xe ^ d, t, r ^ flip))
+        greet((xe ^ d, t, r))
     for b in range(nx):
         @pl.when(jnp.logical_not(jnp.logical_and(here, xe == b)))
         def _():
             greet((b, xe, r))
-
-        @pl.when(jnp.logical_not(jnp.logical_and(here, t == b)))
-        def _():
-            greet((t, b, r))
     for load in first:
         load.wait()
     meta_ref[...] = jnp.concatenate(
         [ids_ref[...].astype(F32), gates_ref[...], jnp.zeros((4, tok), F32)], axis=0)
-    greeted = (nt * nr - 1) + (nx - 1) * nr + 2 * nx
-
-    @pl.when(here)
-    def _():
-        pl.semaphore_wait(barrier, greeted - 2)
-
-    @pl.when(jnp.logical_not(here))
-    def _():
-        pl.semaphore_wait(barrier, greeted)
-
-    for d in range(1, nt):
-        to = lax.rem(t + d, nt)
-        send(req_ref, ag.at[t], ag_s.at[d], ag_r.at[t], (xe, to, r))
+    greeted = (nt * nr - 1) + (nx - 1) + nt
+
+    with jax.named_scope("barr"):
+        @pl.when(here)
+        def _():
+            pl.semaphore_wait(barrier, greeted - 1)
+
+        @pl.when(away)
+        def _():
+            pl.semaphore_wait(barrier, greeted)
+
+    def half(b, k):
+        return xin.at[b, pl.ds(pl.multiple_of(k * feat, feat), feat)]
+
+    for tt in reversed(range(nt)):
+        send_if(jnp.logical_not(jnp.logical_and(here, t == tt)), req_ref, half(xe, r),
+                x_s.at[tt], x_r.at[xe], (t, tt, r))
     for d in range(1, nx):
         send(meta_ref, meta.at[xe], me_s.at[d], me_r.at[xe], (xe ^ d, t, r))
     meta[xe] = meta_ref[...]
 
-    for d in (3, 1, 2, 0):
-        tx = xe ^ d
-        own = tx == t
-
-        @pl.when(jnp.logical_not(own))
-        def _():
-            got(ag.at[tx], ag_s.at[0], ag_r.at[tx])
-        for flip in (0, 1):
-            if d == 0 and flip == 0:
-                continue
-            ss, rs = x_s.at[2 * d + flip], x_r.at[xe, r]
-            dev = (tx, t, r ^ flip)
-            send_if(own, req_ref, xin.at[xe, r], ss, rs, dev)
-            send_if(jnp.logical_not(own), ag.at[tx], xin.at[xe, r], ss, rs, dev)
-
-    is_own = xe == t
-
-    @pl.when(is_own)
+    @pl.when(here)
     def _():
-        xin[xe, r] = req_ref[...]
-
-    @pl.when(jnp.logical_not(is_own))
-    def _():
-        xin[xe, r] = ag[xe]
-
-    for d in range(1, nx):
-        got(meta.at[xe ^ d], me_s.at[0], me_r.at[xe ^ d])
-    for d in range(nx):
-        for flip in range(nr):
-            if d == 0 and flip == 0:
-                continue
-            slot = (xe ^ d, r ^ flip)
-            got(xin.at[slot], x_s.at[0], x_r.at[slot])
-    for b in range(nx):
-        for k in range(nr):
-            xs[b, :, k * feat:(k + 1) * feat] = xin[b, k].T
-    info = [meta[b].T for b in range(nx)]
+        half(xe, r)[...] = req_ref[...]
+
+    with jax.named_scope("xin"):
+        for d in range(nx):
+            b = xe ^ d
+            if d == 0:
+                @pl.when(away)
+                def _():
+                    got(half(b, r), x_s.at[0], x_r.at[b])
+                send_if(here, req_ref, half(b, r), q_s.at[d], q_r.at[b], partner)
+                send_if(away, half(b, r), half(b, r), q_s.at[d], q_r.at[b], partner)
+            else:
+                got(half(b, r), x_s.at[0], x_r.at[b])
+                send(half(b, r), half(b, r), q_s.at[d], q_r.at[b], partner)
+    with jax.named_scope("xpart"):
+        for d in range(1, nx):
+            got(meta.at[xe ^ d], me_s.at[0], me_r.at[xe ^ d])
+        info = [meta[b].T for b in range(nx)]
+        for d in range(nx):
+            b = xe ^ d
+            got(half(b, 1 - r), q_s.at[0], q_r.at[b])
+            xs[b] = xin[b].T
 
     def column(c, j):
         return jnp.concatenate([info[b][c * sub:(c + 1) * sub, j:j + 1] for b in range(nx)], axis=0)
@@ -206,28 +204,28 @@
         low, high = total[:, :feat], total[:, feat:]
         mine[c] = jnp.where(r == 0, low, high).reshape(nx, sub, feat)
         dsend0[c] = jnp.where(r == 0, high, low).astype(BF16).reshape(nx, sub, feat)
-        send(dsend0.at[c], drecv0.at[c], p_s.at[c], p_r.at[c], (xe, t, 1 - r))
+        send(dsend0.at[c], drecv0.at[c], p_s.at[c], p_r.at[c], partner)
 
     def pair_chunk(c):
         got(drecv0.at[c], p_s.at[c], p_r.at[c])
         dsend[c] = (mine[c] + drecv0[c].astype(F32)).astype(BF16)
-        for b in range(nx):
-            self_copy = jnp.logical_and(here, xe == b)
-
-            @pl.when(self_copy)
-            def _():
-                drecv[c, t] = dsend[c, b]
-            send_if(jnp.logical_not(self_copy), dsend.at[c, b], drecv.at[c, t], d_s.at[c, b],
-                    d_r.at[c, t], (b, xe, r))
+        for d in (3, 1, 2):
+            send(dsend.at[c, xe ^ d], gat.at[c, xe], g_s.at[c, d], g_r.at[c, xe], (xe ^ d, t, r))
+        gat[c, xe] = dsend[c, xe]
+        send_if(away, dsend.at[c, xe], zrec.at[c, t], z_s.at[c, 0], z_r.at[c, t], (xe, xe, r))
+
+    def pass_chunk(c):
+        for d in (1, 2, 3):
+            q = xe ^ d
+            got(gat.at[c, q], g_s.at[c, 0], g_r.at[c, q])
+            send_if(q != t, gat.at[c, q], zrec.at[c, t], z_s.at[c, d], z_r.at[c, t], (xe, q, r))
 
     def mixed_chunk(c):
-        for src in range(nt):
-            @pl.when(jnp.logical_not(jnp.logical_and(here, t == src)))
-            def _():
-                got(drecv.at[c, src], d_s.at[c, 0], d_r.at[c, src])
-        total = drecv[c, 0].astype(F32)
-        for src in range(1, nt):
-            total = total + drecv[c, src].astype(F32)
+        total = gat[c, t].astype(F32)
+        for d in range(1, nt):
+            src = t ^ d
+            got(zrec.at[c, src], z_s.at[c, 0], z_r.at[c, src])
+            total = total + zrec[c, src].astype(F32)
         value = total.astype(BF16)
         mixed_rows[c * sub:(c + 1) * sub, :] = value
         part = jnp.dot(value, tin[...], preferred_element_type=F32).astype(BF16)
@@ -239,33 +237,35 @@
                     (xe, to // nr, to % nr))
 
     def both(stage, c):
-        if 0 <= c < CHUNKS:
-            for h in range(2):
-                stage(c, h)
+        for h in range(2):
+            stage(c, h)
 
     def one(stage, c):
-        if 0 <= c < CHUNKS:
-            stage(c)
-
-    for i in range(CHUNKS + 6):
+        stage(c)
+
+    stages = (
+        ("fw", both, forward, 4), ("rb", both, reduce_second, 3), ("ra", both, reduce_first, 2),
+        ("up", one, up_chunk, 0), ("co", both, collect, 5), ("dn", one, down_chunk, 5),
+        ("ps", one, pass_chunk, 6), ("pr", one, pair_chunk, 5), ("mx", one, mixed_chunk, 7),
+    )
+    for i in range(CHUNKS + 7):
         if i == 5:
             for load in loads[1:]:
                 load.wait()
-        both(forward, i - 4)
-        both(reduce_second, i - 3)
-        both(reduce_first, i - 2)
-        one(up_chunk, i)
-        both(collect, i - 5)
-        one(down_chunk, i - 5)
-        one(pair_chunk, i - 6)
-    for c in range(CHUNKS):
-        mixed_chunk(c)
+        if i == CHUNKS + 6:
+            with jax.named_scope("drain"):
+                drain()
+        for name, kind, stage, lag in stages:
+            if 0 <= i - lag < CHUNKS:
+                with jax.named_scope(f"{name}{i - lag}"):
+                    kind(stage, i - lag)
     mixed_ref[...] = mixed_rows[...].T
-    pre = fsend[me].astype(F32)
-    for d in range(1, nt * nr):
-        frm = me ^ d
-        got(frecv.at[frm], f_s.at[0], f_r.at[frm])
-        pre = pre + frecv[frm].astype(F32)
+    with jax.named_scope("fin"):
+        pre = fsend[me].astype(F32)
+        for d in range(1, nt * nr):
+            frm = me ^ d
+            got(frecv.at[frm], f_s.at[0], f_r.at[frm])
+            pre = pre + frecv[frm].astype(F32)
     active = jnp.maximum(pre + bias_ref[...].reshape(1, tasks * th), 0.0)
     outs = []
     for j in range(tasks):
@@ -276,13 +276,8 @@
     for j in range(tasks):
         logits = jnp.where(lane == j, outs[j] + ob_ref[j], logits)
     scores_ref[...] = jax.nn.sigmoid(logits.T[:tasks, :])
-    for cond, copy in started:
-        if cond is None:
-            copy.wait_send()
-        else:
-            @pl.when(cond)
-            def _(copy=copy):
-                copy.wait_send()
+    with jax.named_scope("end"):
+        drain()
 
 
 def stay_device(requests, expert_ids, gate_values, w_up, w_down, tower_in, tower_bias, tower_out,
@@ -305,24 +300,25 @@
         pltpu.VMEM(tower_bias.shape, F32), pltpu.VMEM(tower_out.shape, F32),
         pltpu.VMEM(w_up.shape, BF16), pltpu.VMEM(w_down.shape, BF16),
         pltpu.VMEM(tower_in.shape, BF16),
-        pltpu.VMEM((nt, feat, tok), BF16), pltpu.VMEM((8, tok), F32), pltpu.VMEM((nx, 8, tok), F32),
-        pltpu.VMEM((nx, nr, feat, tok), BF16), pltpu.VMEM((nx, tok, nr * feat), BF16),
+        pltpu.VMEM((8, tok), F32), pltpu.VMEM((nx, 8, tok), F32),
+        pltpu.VMEM((nx, nr * feat, tok), BF16), pltpu.VMEM((nx, tok, nr * feat), BF16),
         pltpu.VMEM((C, 2, nx, 2 * sub, hcols), BF16),
         pltpu.VMEM((C, 2, 2, 2 * sub, hcols), BF16),
         pltpu.VMEM((C, 2, 2 * sub, hcols), BF16), pltpu.VMEM((C, 2, 2 * sub, hcols), BF16),
         pltpu.VMEM((C, 2, nx, 2 * sub, hcols), BF16),
         pltpu.VMEM((C, nx, sub, feat), F32), pltpu.VMEM((C, nx, sub, feat), BF16),
         pltpu.VMEM((C, nx, sub, feat), BF16), pltpu.VMEM((C, nx, sub, feat), BF16),
-        pltpu.VMEM((C, nt, sub, feat), BF16),
+        pltpu.VMEM((C, nx, sub, feat), BF16), pltpu.VMEM((C, nt, sub, feat), BF16),
         pltpu.VMEM((nt * nr, each, tasks * th), BF16), pltpu.VMEM((nt * nr, each, tasks * th), BF16),
         pltpu.VMEM((tok, feat), BF16),
-        dma((8,)), dma((nt,)), dma((nt,)), dma((nx,)), dma((nx,)), dma((2 * nx,)), dma((nx, nr)),
+        dma((8,)), dma((nx,)), dma((nx,)), dma((nt,)), dma((nx,)), dma((nx,)), dma((nx,)),
         dma((C, 2, 2)), dma((C, 2, 2)), dma((C, 2)), dma((C, 2)), dma((C, 2, 3)), dma((C, 2, nx)),
-        dma((C,)), dma((C,)), dma((C, nx)), dma((C, nt)), dma((nt * nr,)), dma((nt * nr,)),
+        dma((C,)), dma((C,)), dma((C, nx)), dma((C, nx)), dma((C, nx)), dma((C, nt)),
+        dma((nt * nr,)), dma((nt * nr,)),
     ]
     mixed, scores = pl.pallas_call(
         functools.partial(stay_kernel, dims),
-        out_shape=(jax.ShapeDtypeStruct((feat, tok), BF16), jax.ShapeDtypeStruct((tasks, each), F32)),
+        out_shape=(pltpu.VMEM((feat, tok), BF16), pltpu.VMEM((tasks, each), F32)),
         in_specs=[hbm] * 8 + [smem],
         out_specs=(vmem, vmem),
         scratch_shapes=scratch,

time: 71.1 us -> 61.3 us (0.86); the launches traced: 70 us -> 61.2 us
  Pallas kernels: 66.7 us -> 59.3 us
  local copies, waits for them, and re-layouts: 2.66 us -> 1.2 us
    pallas_call x1, Pallas kernels: 66.7 us -> 59.3 us  [stay_device(): pl.pallas_call(functools.partial(stay_kernel, dims), out_shape=(pltpu.VME...]
    unnamed x2, local copies, waits for them, and re-layouts: 2.66 us -> 1.2 us
where the time goes in v1:
time: 61.3 us; the launch traced here: 61.2 us
  Pallas kernels  59.3 us (97%)
  local copies, waits for them, and re-layouts  1.2 us (2%)
  between operations  0.64 us (1%)
    pallas_call x1, Pallas kernels, stay_device(): pl.pallas_call(functools.partial(stay_kernel, dims), out_shape=(pltpu.VME...  59.3 us

profile of v1, /device:TPU:25, one launch (start us, length us, event | category | flops | bytes accessed | tf_op | source)
XLA Modules:
  0.0 61.2 jit_solution(10644800891457049033)
XLA Ops:
  0.6 59.3 %stay.1 = (bf16[192,128]{1,0:T(8,128)(2,1)S(1)}, f32[3,16]{1,0:T(4,128)S(1)}) custom-call(bf16[192,128]{1,0:T(8,128)(2,1)} %bitcast.5, s32[2,128]{1,0:T(2,128)} %bitcast.6, f32[2,128]{1,0:T(2,128)} %bitcast.7, bf16[4,384,768]{2,1,0:T(8,128)(2,1)} %up_hbm.1, bf16[4,384,768]{2,1,0:T(8,128)(2,1)} %down_hbm.1, bf16[192,768]{1,0:T(8,128)(2,1)} %tin_hbm.1, ...), custom_call_target="tpu_custom_call" | custom-call | tf_op jit(solution)/shard_map/stay/pallas_call | solution.py:319
  60.0 0.6 %copy.13 = bf16[128,192]{0,1:T(8,128)(2,1)} copy(bf16[128,192]{0,1:T(8,128)(2,1)S(1)} %bitcast.4) | data formatting | bytes 98304
  60.6 0.6 copy.14

commit v2 on v1

v2 whole, which is shorter than its diff:
```python
import functools
import jax
import jax.numpy as jnp
from jax import lax
from jax.experimental import pallas as pl
from jax.experimental.pallas import tpu as pltpu
from jax.sharding import PartitionSpec as P

MESH = pl.DeviceIdType.MESH
F32 = jnp.float32
BF16 = jnp.bfloat16


def stay_kernel(
    dims, req_hbm, ids_hbm, gates_hbm, up_hbm, down_hbm, tin_hbm, bias_hbm, tout_hbm, ob_ref,
    mixed_ref, scores_ref,
    req_ref, ids_ref, gates_ref, bias_ref, tout_ref, up, down, tin, meta_ref, meta, rt, xs,
    hp, r1, s2, r2, hid, mine, dsend0, drecv0, dsend, gat, zrec, fsend, frecv, rows_out,
    lsem, me_s, me_r, x_s, x_r, q_s, q_r, s1_s, s1_r, s2_s, s2_r, h_s, h_r,
    p_s, p_r, g_s, g_r, z_s, z_r, m_s, m_r, t_s, t_r, f_s, f_r,
):
    nx, nt, nr, experts, tok, feat, hcols, tasks, th, unit, sizes = dims
    xe, t, r = lax.axis_index("expert"), lax.axis_index("tensor"), lax.axis_index("rep")
    chunks = len(sizes)
    offs = [sum(sizes[:c]) * unit for c in range(chunks)]
    subs = [n * unit for n in sizes]

    def remote(src, dst, ssem, rsem, dev):
        return pltpu.make_async_remote_copy(
            src_ref=src, dst_ref=dst, send_sem=ssem, recv_sem=rsem, device_id=dev,
            device_id_type=MESH)

    def send(src, dst, ssem, rsem, dev):
        remote(src, dst, ssem, rsem, dev).start()

    def got(ref, rsem):
        remote(ref, ref, lsem.at[0], rsem, (xe, t, r)).wait_recv()

    def sent(ref, ssem):
        remote(ref, ref, ssem, lsem.at[0], (xe, t, r)).wait_send()

    first = [
        pltpu.make_async_copy(req_hbm, req_ref, lsem.at[3]),
        pltpu.make_async_copy(ids_hbm, ids_ref, lsem.at[4]),
        pltpu.make_async_copy(gates_hbm, gates_ref, lsem.at[5]),
    ]

    def own_rows(ref, k):
        return ref.at[pl.ds(pl.multiple_of(k * feat, feat), feat)]

    loads = [
        pltpu.make_async_copy(up_hbm, up, lsem.at[0]),
        pltpu.make_async_copy(down_hbm, down, lsem.at[1]),
        pltpu.make_async_copy(tin_hbm, own_rows(tin, r), lsem.at[2]),
        pltpu.make_async_copy(bias_hbm, bias_ref, lsem.at[6]),
        pltpu.make_async_copy(tout_hbm, tout_ref, lsem.at[7]),
    ]
    for load in first + loads:
        load.start()
    here = t == xe
    away = jnp.logical_not(here)
    partner = (xe, t, 1 - r)
    barrier = pltpu.get_barrier_semaphore()

    def greet(dev):
        pl.semaphore_signal(barrier, inc=1, device_id=dev, device_id_type=MESH)

    me = t * nr + r
    for d in range(1, nt * nr):
        other = me ^ d
        greet((xe, lax.div(other, nr), lax.rem(other, nr)))
    for d in range(1, nx):
        greet((xe ^ d, t, r))
    for b in range(nx):
        @pl.when(jnp.logical_not(jnp.logical_and(here, xe == b)))
        def _():
            greet((b, xe, r))
    for load in first:
        load.wait()
    rt[...] = req_ref[...].T
    meta_ref[...] = jnp.concatenate(
        [ids_ref[...].astype(F32), gates_ref[...], jnp.zeros((4, tok), F32)], axis=0)
    greeted = (nt * nr - 1) + (nx - 1) + nt

    with jax.named_scope("barr"):
        @pl.when(here)
        def _():
            pl.semaphore_wait(barrier, greeted - 1)

        @pl.when(away)
        def _():
            pl.semaphore_wait(barrier, greeted)

    def span(c):
        return pl.ds(offs[c], subs[c])

    for c in range(chunks):
        for tt in reversed(range(nt)):
            @pl.when(jnp.logical_not(jnp.logical_and(here, t == tt)))
            def _():
                send(rt.at[span(c)], xs.at[r, xe, span(c)], x_s, x_r.at[c], (t, tt, r))
        if c == 0:
            for d in range(1, nx):
                send(meta_ref, meta.at[xe], me_s, me_r, (xe ^ d, t, r))
    send(tin_hbm, own_rows(tin, r), t_s, t_r, partner)
    meta[xe] = meta_ref[...]

    @pl.when(here)
    def _():
        xs[r, xe] = rt[...]

    def take(c):
        @pl.when(here)
        def _():
            got(xs.at[r, pl.ds(0, nx - 1), span(c)], x_r.at[c])

        @pl.when(away)
        def _():
            got(xs.at[r, :, span(c)], x_r.at[c])
        send(xs.at[r, :, span(c)], xs.at[r, :, span(c)], q_s, q_r.at[c], partner)

    with jax.named_scope("take0"):
        take(0)
    with jax.named_scope("meta"):
        got(meta.at[pl.ds(0, nx - 1)], me_r)
        info = [meta[b].T for b in range(nx)]

    def column(c, j):
        return jnp.concatenate(
            [info[b][offs[c]:offs[c] + subs[c], j:j + 1] for b in range(nx)], axis=0)

    near = (1, 2)

    def picks(c, k=None):
        if k is None:
            return pl.ds(2 * offs[c], 2 * subs[c])
        return pl.ds(2 * offs[c] + k * subs[c], subs[c])

    def up_chunk(c):
        sub = subs[c]
        if c + 1 < chunks:
            take(c + 1)
        got(xs.at[1 - r, :, span(c)], q_r.at[c])
        if c == 0:
            loads[0].wait()
        rows = [xs[k, :, offs[c]:offs[c] + sub, :].reshape(nx * sub, feat) for k in range(nr)]
        ids = (column(c, 0), column(c, 1))
        for h in range(2):
            picked = [jnp.zeros((nx * sub, hcols), F32)] * 2
            for e in range(experts):
                part = None
                for k in range(nr):
                    one = jnp.dot(rows[k], up[e, k * feat:(k + 1) * feat, h * hcols:(h + 1) * hcols],
                                  preferred_element_type=F32)
                    part = one if part is None else part + one
                picked = [jnp.where(ids[k] == float(e), part, picked[k]) for k in range(2)]
            for k in range(2):
                hp[h, :, picks(c, k), :] = picked[k].astype(BF16).reshape(nx, sub, hcols)
            fa, fb = near[h], near[1 - h]
            for i, q in enumerate((xe ^ fa ^ fb, xe ^ fa)):
                send(hp.at[h, q, picks(c)], r1.at[h, i, picks(c)], s1_s, s1_r.at[c, h, i],
                     (xe ^ fa, t, r))

    def reduce_first(c, h):
        fa, fb = near[h], near[1 - h]
        got(r1.at[h, 0, picks(c)], s1_r.at[c, h, 0])
        s2[h, picks(c)] = (hp[h, xe ^ fb, picks(c)].astype(F32)
                           + r1[h, 0, picks(c)].astype(F32)).astype(BF16)
        send(s2.at[h, picks(c)], r2.at[h, picks(c)], s2_s, s2_r.at[c, h], (xe ^ fb, t, r))

    def reduce_second(c, h):
        fa, fb = near[h], near[1 - h]
        got(r1.at[h, 1, picks(c)], s1_r.at[c, h, 1])
        got(r2.at[h, picks(c)], s2_r.at[c, h])
        total = (hp[h, xe, picks(c)].astype(F32) + r1[h, 1, picks(c)].astype(F32)
                 + r2[h, picks(c)].astype(F32))
        hid[h, xe, picks(c)] = jnp.maximum(total, 0.0).astype(BF16)
        mine_ref = hid.at[h, xe, picks(c)]
        send(mine_ref, mine_ref, h_s.at[0], h_r.at[c, h, 0], (xe ^ fb, t, r))
        send(mine_ref, mine_ref, h_s.at[0], h_r.at[c, h, 1], (xe ^ fa, t, r))

    def forward(c, h):
        fa, fb = near[h], near[1 - h]
        ref = hid.at[h, xe ^ fb, picks(c)]
        got(ref, h_r.at[c, h, 0])
        send(ref, ref, h_s.at[1], h_r.at[c, h, 2], (xe ^ fa, t, r))

    def collect(c, h):
        fa, fb = near[h], near[1 - h]
        got(hid.at[h, xe ^ fa, picks(c)], h_r.at[c, h, 1])
        got(hid.at[h, xe ^ fa ^ fb, picks(c)], h_r.at[c, h, 2])

    def parity(c):
        return sum(sizes[:c]) % nr if sizes[c] == 1 else None

    def slot(c, core):
        return (sum(sizes[:c]) + (sizes[c] - 1 if sizes[c] > 1 else 0)) // nr - (
            core if sizes[c] > 1 else 0)

    def if_core(c, other, body):
        p = parity(c)
        if p is None:
            body()
        else:
            pl.when(r == (1 - p if other else p))(body)

    def down_chunk(c):
        sub = subs[c]
        ids = (column(c, 0), column(c, 1))
        gates = (column(c, 2), column(c, 3))
        total = jnp.zeros((nx * sub, nr * feat), F32)
        for e in range(experts):
            hit = (ids[0] == float(e), ids[1] == float(e))
            weight = jnp.where(hit[0], gates[0], 0.0) + jnp.where(hit[1], gates[1], 0.0)
            part = None
            for h in range(2):
                values = [hid[h, :, picks(c, k), :].reshape(nx * sub, hcols) for k in range(2)]
                chosen = jnp.where(hit[0], values[0], jnp.where(hit[1], values[1], jnp.zeros_like(values[1])))
                one = lax.dot_general(chosen, down[e, :, h * hcols:(h + 1) * hcols],
                                      (((1,), (1,)), ((), ())), preferred_element_type=F32)
                part = one if part is None else part + one
            total = total + weight * part
        total = total.reshape(nx, sub, nr * feat)
        if sizes[c] == 1:
            keep = give = total
        else:
            odd, even = total[:, :unit], total[:, unit:]
            keep = jnp.where(r == 0, even, odd)
            give = jnp.where(r == 0, odd, even)

        def store():
            mine[slot(c, r)] = keep

        def give_away():
            at = slot(c, 1 - r)
            dsend0[c] = give.astype(BF16)
            send(dsend0.at[c], drecv0.at[at], p_s, p_r.at[at], partner)
        if_core(c, True, give_away)
        if_core(c, False, store)

    def pair_chunk(c):
        def body():
            s = slot(c, r)
            got(drecv0.at[s], p_r.at[s])
            dsend[s] = (mine[s] + drecv0[s].astype(F32)).astype(BF16)
            for d in (3, 1, 2):
                send(dsend.at[s, xe ^ d], gat.at[s, xe], g_s, g_r.at[s, d - 1], (xe ^ d, t, r))
            gat[s, xe] = dsend[s, xe]

            @pl.when(away)
            def _():
                send(dsend.at[s, xe], zrec.at[s, t], z_s, z_r.at[s], (xe, xe, r))
        if_core(c, False, body)

    def pass_chunk(c):
        def body():
            s = slot(c, r)
            for d in (1, 2, 3):
                q = xe ^ d
                got(gat.at[s, q], g_r.at[s, d - 1])

                @pl.when(q != t)
                def _():
                    send(gat.at[s, q], zrec.at[s, t], z_s, z_r.at[s], (xe, q, r))
        if_core(c, False, body)

    def mixed_chunk(c):
        def body():
            s = slot(c, r)
            got(zrec.at[s, pl.ds(0, nt - 1)], z_r.at[s])
            total = gat[s, t].astype(F32)
            for d in range(1, nt):
                total = total + zrec[s, t ^ d].astype(F32)
            value = total.astype(BF16)
            at = pl.ds(pl.multiple_of((s * nr + r) * unit, unit), unit)
            rows_out[at, :] = value
            send(rows_out.at[at], rows_out.at[at], m_s, m_r, partner)
            fsend[s] = jnp.dot(value, tin[...], preferred_element_type=F32).astype(BF16)

            @pl.when(t != s)
            def _():
                send(fsend.at[s], frecv.at[t], f_s, f_r, (xe, s, r))
        if_core(c, False, body)

    def both(stage, c):
        for h in range(2):
            stage(c, h)

    def one(stage, c):
        stage(c)

    stages = (
        ("fw", both, forward, 4), ("rb", both, reduce_second, 3), ("ra", both, reduce_first, 2),
        ("up", one, up_chunk, 0), ("co", both, collect, 5), ("dn", one, down_chunk, 5),
        ("ps", one, pass_chunk, 6), ("pr", one, pair_chunk, 5), ("mx", one, mixed_chunk, 7),
    )
    for i in range(chunks + 7):
        if i == 5:
            for load in loads[1:]:
                load.wait()
            got(own_rows(tin, 1 - r), t_r)
        if i == chunks + 6:
            with jax.named_scope("drain"):
                sent(r1, s1_s)
                sent(r2, s2_s)
                sent(r1, h_s.at[0])
                sent(r2, h_s.at[1])
                sent(meta.at[pl.ds(0, nx - 1)], me_s)
                sent(own_rows(tin, r), t_s)
                sent(xs.at[r], q_s)
                sent(drecv0, p_s)
                sent(gat.at[:, pl.ds(0, nx - 1)], g_s)

                @pl.when(here)
                def _():
                    sent(xs.at[r, pl.ds(0, nx - 1)], x_s)

                @pl.when(away)
                def _():
                    sent(xs.at[r], x_s)
        for name, kind, stage, lag in stages:
            if 0 <= i - lag < chunks:
                with jax.named_scope(f"{name}{i - lag}"):
                    kind(stage, i - lag)
    half = tok // nr
    with jax.named_scope("mout"):
        got(rows_out.at[pl.ds(0, half)], m_r)
    out = rows_out[...].T
    mixed_ref[...] = jnp.where(r == 0, out[:feat], out[feat:])
    with jax.named_scope("fin"):
        got(frecv.at[pl.ds(0, nt - 1)], f_r)
        pre = fsend[t].astype(F32)
        for d in range(1, nt):
            pre = pre + frecv[t ^ d].astype(F32)
    active = jnp.maximum(pre + bias_ref[...].reshape(1, tasks * th), 0.0)
    outs = []
    for j in range(tasks):
        outs.append(jnp.sum(active[:, j * th:(j + 1) * th] * tout_ref[j:j + 1, :], axis=1, keepdims=True))
    lane = lax.broadcasted_iota(jnp.int32, (unit, 128), 1)
    logits = jnp.zeros((unit, 128), F32)
    for j in range(tasks):
        logits = jnp.where(lane == j, outs[j] + ob_ref[j], logits)
    scores_ref[...] = jax.nn.sigmoid(logits.T[:tasks, :])
    with jax.named_scope("end"):
        sent(zrec.at[:, pl.ds(0, nt - 1)], z_s)
        sent(rows_out.at[pl.ds(0, half)], m_s)
        sent(frecv.at[pl.ds(0, nt - 1)], f_s)


def stay_device(requests, expert_ids, gate_values, w_up, w_down, tower_in, tower_bias, tower_out,
                out_bias):
    nx, nt, nr = lax.axis_size("expert"), lax.axis_size("tensor"), lax.axis_size("rep")
    experts, _, hid_cols = w_up.shape
    tok, feat = requests.shape
    tasks, th = tower_out.shape
    hcols = hid_cols // 2
    unit = tok // (nt * nr)
    sizes = (1,) + (nr,) * (nt - 1) + (1,)
    C = len(sizes)
    dims = (nx, nt, nr, experts, tok, feat, hcols, tasks, th, unit, sizes)
    vmem = pl.BlockSpec(memory_space=pltpu.VMEM)
    hbm = pl.BlockSpec(memory_space=pltpu.HBM)
    smem = pl.BlockSpec(memory_space=pltpu.SMEM)
    dma = pltpu.SemaphoreType.DMA
    wide = nr * feat
    scratch = [
        pltpu.VMEM((feat, tok), BF16), pltpu.VMEM((2, tok), jnp.int32), pltpu.VMEM((2, tok), F32),
        pltpu.VMEM(tower_bias.shape, F32), pltpu.VMEM(tower_out.shape, F32),
        pltpu.VMEM(w_up.shape, BF16), pltpu.VMEM(w_down.shape, BF16),
        pltpu.VMEM((wide, tower_in.shape[1]), BF16),
        pltpu.VMEM((8, tok), F32), pltpu.VMEM((nx, 8, tok), F32),
        pltpu.VMEM((tok, feat), BF16), pltpu.VMEM((nr, nx, tok, feat), BF16),
        pltpu.VMEM((2, nx, 2 * tok, hcols), BF16),
        pltpu.VMEM((2, 2, 2 * tok, hcols), BF16),
        pltpu.VMEM((2, 2 * tok, hcols), BF16), pltpu.VMEM((2, 2 * tok, hcols), BF16),
        pltpu.VMEM((2, nx, 2 * tok, hcols), BF16),
        pltpu.VMEM((nt, nx, unit, wide), F32), pltpu.VMEM((C, nx, unit, wide), BF16),
        pltpu.VMEM((nt, nx, unit, wide), BF16), pltpu.VMEM((nt, nx, unit, wide), BF16),
        pltpu.VMEM((nt, nx, unit, wide), BF16), pltpu.VMEM((nt, nt, unit, wide), BF16),
        pltpu.VMEM((nt, unit, tasks * th), BF16), pltpu.VMEM((nt, unit, tasks * th), BF16),
        pltpu.VMEM((tok, wide), BF16),
        dma((8,)), dma, dma, dma, dma((C,)), dma, dma((C,)),
        dma, dma((C, 2, 2)), dma, dma((C, 2)), dma((2,)), dma((C, 2, 3)),
        dma, dma((nt,)), dma, dma((nt, nx - 1)), dma, dma((nt,)), dma, dma, dma, dma, dma, dma,
    ]
    mixed, scores = pl.pallas_call(
        functools.partial(stay_kernel, dims),
        out_shape=(pltpu.VMEM((feat, tok), BF16), pltpu.VMEM((tasks, unit), F32)),
        in_specs=[hbm] * 8 + [smem],
        out_specs=(vmem, vmem),
        scratch_shapes=scratch,
        compiler_params=pltpu.CompilerParams(
            has_side_effects=True, collective_id=0, vmem_limit_bytes=60 << 20),
        name="stay",
    )(requests.T, expert_ids.T, gate_values.T, w_up, w_down, tower_in, tower_bias, tower_out, out_bias)
    return mixed.T, scores


def weights_stay(mesh):
    return mesh.shape["expert"] == 4 and mesh.shape["tensor"] == 4 and mesh.shape["rep"] == 2


def tower_head(pre, tower_bias, tower_out, out_bias):
    active = jax.nn.relu(pre + tower_bias[None, :])
    active = active.reshape(pre.shape[0], tower_out.shape[0], tower_out.shape[1])
    logits = jnp.sum(active * tower_out[None, :, :], axis=2) + out_bias[None, :]
    return jax.nn.sigmoid(logits).T


def per_device(
    requests, expert_ids, gate_values, w_up, w_down, tower_in, tower_bias, tower_out, out_bias
):
    groups = lax.axis_size("expert")
    experts = w_up.shape[0]
    local_experts = experts // groups
    tok_rows = requests.shape[0]
    capacity = 3 * tok_rows // experts
    serve_up, serve_down = (
        lax.all_to_all(w_up, "expert", split_axis=0, concat_axis=1, tiled=True),
        lax.all_to_all(w_down, "expert", split_axis=0, concat_axis=1, tiled=True),
    )
    flat_ids = expert_ids.reshape(-1)
    onehot = (flat_ids[:, None] == jnp.arange(experts, dtype=jnp.int32)[None, :]).astype(jnp.int32)
    before = jnp.cumsum(onehot, axis=0) - onehot
    slot_rank = jnp.sum(before * onehot, axis=1)
    slots = (flat_ids * capacity + slot_rank).reshape(tok_rows, 2)
    slot_index = jnp.arange(experts * capacity, dtype=jnp.int32)
    spread = (
        (slot_index[:, None] == slots[None, :, 0]) | (slot_index[:, None] == slots[None, :, 1])
    ).astype(jnp.bfloat16)
    full_rows = lax.all_gather(requests, ("tensor", "rep"), axis=1, tiled=True)
    outgoing = jnp.dot(spread, full_rows, preferred_element_type=jnp.float32).astype(jnp.bfloat16)
    incoming = lax.all_to_all(outgoing, "expert", split_axis=0, concat_axis=0, tiled=True)
    shaped = incoming.reshape(groups, local_experts, capacity, incoming.shape[1])
    hidden_pre = jnp.einsum("secd,edh->sech", shaped, serve_up, preferred_element_type=jnp.float32)
    hidden = jax.nn.relu(hidden_pre).astype(jnp.bfloat16)
    partial_value = jnp.einsum(
        "sech,edh->secd", hidden, serve_down, preferred_element_type=jnp.float32
    )
    summed = lax.psum_scatter(
        partial_value.astype(jnp.bfloat16), ("tensor", "rep"), scatter_dimension=3, tiled=True
    ).astype(jnp.float32)
    expert_out = summed.astype(jnp.bfloat16).reshape(
        groups * local_experts * capacity, summed.shape[3]
    )
    returned = lax.all_to_all(expert_out, "expert", split_axis=0, concat_axis=0, tiled=True)
    pick_first = (slots[:, 0:1] == slot_index[None, :]).astype(jnp.bfloat16)
    pick_second = (slots[:, 1:2] == slot_index[None, :]).astype(jnp.bfloat16)
    first = jnp.dot(pick_first, returned, preferred_element_type=jnp.float32)
    second = jnp.dot(pick_second, returned, preferred_element_type=jnp.float32)
    mixed = (gate_values[:, 0:1] * first + gate_values[:, 1:2] * second).astype(jnp.bfloat16)
    pre = lax.psum_scatter(
        jnp.dot(mixed, tower_in, preferred_element_type=jnp.float32).astype(jnp.bfloat16),
        ("tensor", "rep"),
        scatter_dimension=0,
        tiled=True,
    ).astype(jnp.float32)
    scores = tower_head(pre, tower_bias, tower_out, out_bias)
    return (mixed, scores)


def solution(mesh):
    in_specs = (
        P("expert", ("tensor", "rep")),
        P("expert", None),
        P("expert", None),
        P(None, "expert", ("tensor", "rep")),
        P(None, "expert", ("tensor", "rep")),
        P(("tensor", "rep"), None),
        P(),
        P(),
        P(),
    )
    out_specs = (P("expert", ("tensor", "rep")), P(None, ("expert", "tensor", "rep")))
    body = stay_device if weights_stay(mesh) else per_device
    return jax.shard_map(
        body, mesh=mesh, in_specs=in_specs, out_specs=out_specs, check_vma=False
    )
```

time: 61.3 us -> 55.8 us (0.910)
  Pallas kernels: 59.3 us -> 53.4 us
    pallas_call x1, Pallas kernels: 59.3 us -> 53.4 us  [stay_device(): pl.pallas_call(functools.partial(stay_kernel, dims), out_shape=(pltpu.VME...]
where the time goes in v2:
time: 55.8 us; the launch traced here: 55.3 us
  Pallas kernels  53.4 us (96%)
  local copies, waits for them, and re-layouts  1.2 us (2%)
  between operations  0.64 us (1%)
    pallas_call x1, Pallas kernels, stay_device(): pl.pallas_call(functools.partial(stay_kernel, dims), out_shape=(pltpu.VME...  53.4 us
    unnamed x2, local copies, waits for them, and re-layouts  1.2 us

profile of v2, /device:TPU:25, one launch (start us, length us, event | category | flops | bytes accessed | tf_op | source)
XLA Modules:
  0.0 55.3 jit_solution(13493171532628874680)
XLA Ops:
  0.6 53.4 %stay.1 = (bf16[192,128]{1,0:T(8,128)(2,1)S(1)}, f32[3,16]{1,0:T(4,128)S(1)}) custom-call(bf16[192,128]{1,0:T(8,128)(2,1)} %bitcast.5, s32[2,128]{1,0:T(2,128)} %bitcast.6, f32[2,128]{1,0:T(2,128)} %bitcast.7, bf16[4,384,768]{2,1,0:T(8,128)(2,1)} %up_hbm.1, bf16[4,384,768]{2,1,0:T(8,128)(2,1)} %down_hbm.1, bf16[192,768]{1,0:T(8,128)(2,1)} %tin_hbm.1, ...), custom_call_target="tpu_custom_call" | custom-call | tf_op jit(solution)/shard_map/stay/pallas_call | solution.py:386
  54.1 0.6 %copy.13 = bf16[128,192]{0,1:T(8,128)(2,1)} copy(bf16[128,192]{0,1:T(8,128)(2,1)S(1)} %bitcast.4) | data formatting | bytes 98304
  54.7 0.6 %copy.14 = f32[3,16]{1,0:T(4,128)} copy(f32[3,16]{1,0:T(4,128)S(1)} %get-tuple-element.7) | data formatting | bytes 384

commit v3 on v2

--- a/solution.py
+++ b/solution.py
@@ -15,9 +15,9 @@
     dims, req_hbm, ids_hbm, gates_hbm, up_hbm, down_hbm, tin_hbm, bias_hbm, tout_hbm, ob_ref,
     mixed_ref, scores_ref,
     req_ref, ids_ref, gates_ref, bias_ref, tout_ref, up, down, tin, meta_ref, meta, rt, xs,
-    hp, r1, s2, r2, hid, mine, dsend0, drecv0, dsend, gat, zrec, fsend, frecv, rows_out,
+    hp, r1, s2, r2, hid, mine, dsend0, drecv0, dsend, gat, zrec, fsend, frecv, rows_out, lrec, lsum, zl,
     lsem, me_s, me_r, x_s, x_r, q_s, q_r, s1_s, s1_r, s2_s, s2_r, h_s, h_r,
-    p_s, p_r, g_s, g_r, z_s, z_r, m_s, m_r, t_s, t_r, f_s, f_r,
+    p_s, p_r, g_s, g_r, z_s, z_r, m_s, m_r, t_s, t_r, f_s, f_r, l_s, l_r, zl_s, zl_r,
 ):
     nx, nt, nr, experts, tok, feat, hcols, tasks, th, unit, sizes = dims
     xe, t, r = lax.axis_index("expert"), lax.axis_index("tensor"), lax.axis_index("rep")
@@ -55,8 +55,7 @@
         pltpu.make_async_copy(bias_hbm, bias_ref, lsem.at[6]),
         pltpu.make_async_copy(tout_hbm, tout_ref, lsem.at[7]),
     ]
-    for load in first + loads:
-        load.start()
+    first[0].start()
     here = t == xe
     away = jnp.logical_not(here)
     partner = (xe, t, 1 - r)
@@ -66,21 +65,21 @@
         pl.semaphore_signal(barrier, inc=1, device_id=dev, device_id_type=MESH)
 
     me = t * nr + r
-    for d in range(1, nt * nr):
+    for d in reversed(range(1, nt * nr)):
         other = me ^ d
         greet((xe, lax.div(other, nr), lax.rem(other, nr)))
     for d in range(1, nx):
-        greet((xe ^ d, t, r))
+        for k in range(nr):
+            greet((xe ^ d, t, k))
     for b in range(nx):
         @pl.when(jnp.logical_not(jnp.logical_and(here, xe == b)))
         def _():
             greet((b, xe, r))
-    for load in first:
-        load.wait()
+    for load in first[1:] + loads:
+        load.start()
+    first[0].wait()
     rt[...] = req_ref[...].T
-    meta_ref[...] = jnp.concatenate(
-        [ids_ref[...].astype(F32), gates_ref[...], jnp.zeros((4, tok), F32)], axis=0)
-    greeted = (nt * nr - 1) + (nx - 1) + nt
+    greeted = (nt * nr - 1) + (nx - 1) * nr + nt
 
     with jax.named_scope("barr"):
         @pl.when(here)
@@ -100,6 +99,10 @@
             def _():
                 send(rt.at[span(c)], xs.at[r, xe, span(c)], x_s, x_r.at[c], (t, tt, r))
         if c == 0:
+            for load in first[1:]:
+                load.wait()
+            meta_ref[...] = jnp.concatenate(
+                [ids_ref[...].astype(F32), gates_ref[...], jnp.zeros((4, tok), F32)], axis=0)
             for d in range(1, nx):
                 send(meta_ref, meta.at[xe], me_s, me_r, (xe ^ d, t, r))
     send(tin_hbm, own_rows(tin, r), t_s, t_r, partner)
@@ -138,8 +141,6 @@
 
     def up_chunk(c):
         sub = subs[c]
-        if c + 1 < chunks:
-            take(c + 1)
         got(xs.at[1 - r, :, span(c)], q_r.at[c])
         if c == 0:
             loads[0].wait()
@@ -157,21 +158,22 @@
             for k in range(2):
                 hp[h, :, picks(c, k), :] = picked[k].astype(BF16).reshape(nx, sub, hcols)
             fa, fb = near[h], near[1 - h]
-            for i, q in enumerate((xe ^ fa ^ fb, xe ^ fa)):
-                send(hp.at[h, q, picks(c)], r1.at[h, i, picks(c)], s1_s, s1_r.at[c, h, i],
+            for i, q, sem in ((0, xe ^ fa ^ fb, s1_r), (1, xe ^ fa, s2_r)):
+                send(hp.at[h, q, picks(c)], r1.at[h, i, picks(c)], s1_s, sem.at[c, h],
                      (xe ^ fa, t, r))
+        if c + 1 < chunks:
+            take(c + 1)
 
     def reduce_first(c, h):
         fa, fb = near[h], near[1 - h]
-        got(r1.at[h, 0, picks(c)], s1_r.at[c, h, 0])
+        got(r1.at[h, 0, picks(c)], s1_r.at[c, h])
         s2[h, picks(c)] = (hp[h, xe ^ fb, picks(c)].astype(F32)
                            + r1[h, 0, picks(c)].astype(F32)).astype(BF16)
         send(s2.at[h, picks(c)], r2.at[h, picks(c)], s2_s, s2_r.at[c, h], (xe ^ fb, t, r))
 
     def reduce_second(c, h):
         fa, fb = near[h], near[1 - h]
-        got(r1.at[h, 1, picks(c)], s1_r.at[c, h, 1])
-        got(r2.at[h, picks(c)], s2_r.at[c, h])
+        got(r1.at[h, :, picks(c)], s2_r.at[c, h])
         total = (hp[h, xe, picks(c)].astype(F32) + r1[h, 1, picks(c)].astype(F32)
                  + r2[h, picks(c)].astype(F32))
         hid[h, xe, picks(c)] = jnp.maximum(total, 0.0).astype(BF16)
@@ -183,12 +185,14 @@
         fa, fb = near[h], near[1 - h]
         ref = hid.at[h, xe ^ fb, picks(c)]
         got(ref, h_r.at[c, h, 0])
-        send(ref, ref, h_s.at[1], h_r.at[c, h, 2], (xe ^ fa, t, r))
+        send(ref, ref, h_s.at[1], h_r.at[c, h, 1], (xe ^ fa, t, r))
 
     def collect(c, h):
-        fa, fb = near[h], near[1 - h]
-        got(hid.at[h, xe ^ fa, picks(c)], h_r.at[c, h, 1])
-        got(hid.at[h, xe ^ fa ^ fb, picks(c)], h_r.at[c, h, 2])
+        got(hid.at[h, pl.ds(0, 2), picks(c)], h_r.at[c, h, 1])
+
+    last = chunks - 1
+    end_core = (sum(sizes) - 1) % nr
+    final_rows = pl.ds((sum(sizes) - 1) * unit, unit)
 
     def parity(c):
         return sum(sizes[:c]) % nr if sizes[c] == 1 else None
@@ -197,11 +201,14 @@
         return (sum(sizes[:c]) + (sizes[c] - 1 if sizes[c] > 1 else 0)) // nr - (
             core if sizes[c] > 1 else 0)
 
-    def if_core(c, other, body):
+    def if_core(c, other, body, only=None):
         p = parity(c)
         if p is None:
-            body()
-        else:
+            if only is None:
+                body()
+            else:
+                pl.when(r == only)(body)
+        elif only is None or only == p:
             pl.when(r == (1 - p if other else p))(body)
 
     def down_chunk(c):
@@ -221,6 +228,19 @@
                 part = one if part is None else part + one
             total = total + weight * part
         total = total.reshape(nx, sub, nr * feat)
+        if c == last:
+            dsend0[c] = total.astype(BF16)
+            for d in (3, 1, 2):
+                send(dsend0.at[c, xe ^ d], lrec.at[r, xe], l_s, l_r.at[d], (xe ^ d, t, end_core))
+
+            @pl.when(r == end_core)
+            def _():
+                lrec[r, xe] = dsend0[c, xe]
+
+            @pl.when(r != end_core)
+            def _():
+                send(dsend0.at[c, xe], lrec.at[r, xe], l_s, l_r.at[0], partner)
+            return
         if sizes[c] == 1:
             keep = give = total
         else:
@@ -238,33 +258,93 @@
         if_core(c, True, give_away)
         if_core(c, False, store)
 
-    def pair_chunk(c):
+    def last_sum(q):
+        lsum[q] = (lrec[0, q].astype(F32) + lrec[1, q].astype(F32)).astype(BF16)
+        send(lsum.at[q], zl.at[t], zl_s.at[0], zl_r, (xe, q, 1 - r))
+
+        @pl.when(q != t)
+        def _():
+            send(lsum.at[q], zl.at[t], zl_s.at[1], zl_r, (xe, q, r))
+
+        @pl.when(q == t)
+        def _():
+            zl[t] = lsum[q]
+
+    def last_own(c):
+        @pl.when(r == end_core)
+        def _():
+            got(lrec.at[1 - r, xe], l_r.at[0])
+            last_sum(xe)
+
+    def last_pass():
+        for k in reversed(range(nt)):
+            q = t ^ k
+
+            @pl.when(q != xe)
+            def _():
+                got(lrec.at[:, q], l_r.at[q ^ xe])
+                last_sum(q)
+
+    def last_mixed():
+        @pl.when(r == end_core)
+        def _():
+            got(zl.at[pl.ds(0, nt - 1)], zl_r)
+
+        @pl.when(r != end_core)
+        def _():
+            got(zl, zl_r)
+        total = zl[0].astype(F32)
+        for src in range(1, nt):
+            total = total + zl[src].astype(F32)
+        value = total.astype(BF16)
+        rows_out[final_rows, :] = value
+
+        @pl.when(r == end_core)
+        def _():
+            s = nt - 1
+            fsend[s] = jnp.dot(value, tin[...], preferred_element_type=F32).astype(BF16)
+
+            @pl.when(t != s)
+            def _():
+                send(fsend.at[s], frecv.at[t], f_s, f_r, (xe, s, r))
+
+    def pair_chunk(c, only=None):
+        if c == last:
+            return
+
         def body():
             s = slot(c, r)
             got(drecv0.at[s], p_r.at[s])
             dsend[s] = (mine[s] + drecv0[s].astype(F32)).astype(BF16)
             for d in (3, 1, 2):
-                send(dsend.at[s, xe ^ d], gat.at[s, xe], g_s, g_r.at[s, d - 1], (xe ^ d, t, r))
+                send(dsend.at[s, xe ^ d], gat.at[s, xe], g_s, g_r.at[s], (xe ^ d, t, r))
             gat[s, xe] = dsend[s, xe]
 
             @pl.when(away)
             def _():
                 send(dsend.at[s, xe], zrec.at[s, t], z_s, z_r.at[s], (xe, xe, r))
-        if_core(c, False, body)
-
-    def pass_chunk(c):
+        if_core(c, False, body, only)
+
+    def pass_chunk(c, only=None):
+        if c == last:
+            pl.when(r == end_core)(last_pass)
+            return
+
         def body():
             s = slot(c, r)
+            got(gat.at[s, pl.ds(0, nx - 1)], g_r.at[s])
             for d in (1, 2, 3):
                 q = xe ^ d
-                got(gat.at[s, q], g_r.at[s, d - 1])
 
                 @pl.when(q != t)
                 def _():
                     send(gat.at[s, q], zrec.at[s, t], z_s, z_r.at[s], (xe, q, r))
-        if_core(c, False, body)
-
-    def mixed_chunk(c):
+        if_core(c, False, body, only)
+
+    def mixed_chunk(c, only=None):
+        if c == last:
+            return last_mixed()
+
         def body():
             s = slot(c, r)
             got(zrec.at[s, pl.ds(0, nt - 1)], z_r.at[s])
@@ -280,51 +360,78 @@
             @pl.when(t != s)
             def _():
                 send(fsend.at[s], frecv.at[t], f_s, f_r, (xe, s, r))
-        if_core(c, False, body)
-
-    def both(stage, c):
-        for h in range(2):
-            stage(c, h)
-
-    def one(stage, c):
-        stage(c)
-
-    stages = (
-        ("fw", both, forward, 4), ("rb", both, reduce_second, 3), ("ra", both, reduce_first, 2),
-        ("up", one, up_chunk, 0), ("co", both, collect, 5), ("dn", one, down_chunk, 5),
-        ("ps", one, pass_chunk, 6), ("pr", one, pair_chunk, 5), ("mx", one, mixed_chunk, 7),
-    )
-    for i in range(chunks + 7):
-        if i == 5:
+        if_core(c, False, body, only)
+
+    def drain(c):
+        sent(r1, s1_s)
+        sent(r2, s2_s)
+        sent(r1, h_s.at[0])
+        sent(r2, h_s.at[1])
+        sent(meta.at[pl.ds(0, nx - 1)], me_s)
+        sent(own_rows(tin, r), t_s)
+        sent(xs.at[r], q_s)
+
+        @pl.when(r == end_core)
+        def _():
+            sent(lrec.at[0, pl.ds(0, nx - 1)], l_s)
+            sent(drecv0, p_s)
+            sent(gat.at[pl.ds(0, nt - 1), pl.ds(0, nx - 1)], g_s)
+            sent(zrec.at[pl.ds(0, nt - 1), pl.ds(0, nt - 1)], z_s)
+
+        @pl.when(r != end_core)
+        def _():
+            sent(lrec.at[0], l_s)
+            sent(drecv0.at[pl.ds(0, nt - 1)], p_s)
+            sent(gat.at[:, pl.ds(0, nx - 1)], g_s)
+            sent(zrec.at[:, pl.ds(0, nt - 1)], z_s)
+
+        @pl.when(here)
+        def _():
+            sent(xs.at[r, pl.ds(0, nx - 1)], x_s)
+
+        @pl.when(away)
+        def _():
+            sent(xs.at[r], x_s)
+
+    stages = {
+        "fw": forward, "rb": reduce_second, "ra": reduce_first, "up": up_chunk, "co": collect,
+        "dn": down_chunk, "pr": pair_chunk, "ps": pass_chunk, "mx": mixed_chunk, "drain": drain,
+        "pe": last_own,
+    }
+    for core in range(nr):
+        for name in ("pr", "ps", "mx"):
+            stages[f"{name}{core}"] = functools.partial(stages[name], only=core)
+    order = []
+    for i in range(chunks + 4):
+        order += [("up", i), ("ra", i - 1), ("rb", i - 2), ("fw", i - 3), ("co", i - 4), ("dn", i - 4)]
+        if i < chunks + 3:
+            order += [("pr0", i - 4), ("pr1", i - 5), ("ps0", i - 5), ("ps1", i - 6), ("mx0", i - 6), ("mx1", i - 7)]
+    n = last
+    order += [("pr1", n - 1), ("ps0", n - 1), ("ps1", n - 2), ("mx0", n - 2), ("mx1", n - 3),
+              ("ps1", n - 1), ("pe", n), ("mx1", n - 2), ("ps", n), ("mx0", n - 1), ("mx1", n - 1), ("drain", n), ("mx", n)]
+    for name, c in order:
+        if not 0 <= c < chunks or (c == last and name[-1].isdigit()):
+            continue
+        if name == "dn" and c == 0:
             for load in loads[1:]:
                 load.wait()
             got(own_rows(tin, 1 - r), t_r)
-        if i == chunks + 6:
-            with jax.named_scope("drain"):
-                sent(r1, s1_s)
-                sent(r2, s2_s)
-                sent(r1, h_s.at[0])
-                sent(r2, h_s.at[1])
-                sent(meta.at[pl.ds(0, nx - 1)], me_s)
-                sent(own_rows(tin, r), t_s)
-                sent(xs.at[r], q_s)
-                sent(drecv0, p_s)
-                sent(gat.at[:, pl.ds(0, nx - 1)], g_s)
-
-                @pl.when(here)
-                def _():
-                    sent(xs.at[r, pl.ds(0, nx - 1)], x_s)
-
-                @pl.when(away)
-                def _():
-                    sent(xs.at[r], x_s)
-        for name, kind, stage, lag in stages:
-            if 0 <= i - lag < chunks:
-                with jax.named_scope(f"{name}{i - lag}"):
-                    kind(stage, i - lag)
+        with jax.named_scope(f"{name}_{c}"):
+            if name in ("fw", "rb", "ra", "co"):
+                for h in range(2):
+                    stages[name](c, h)
+            else:
+                stages[name](c)
     half = tok // nr
+    fewer = half - unit
     with jax.named_scope("mout"):
-        got(rows_out.at[pl.ds(0, half)], m_r)
+        @pl.when(r == end_core)
+        def _():
+            got(rows_out.at[pl.ds(0, half)], m_r)
+
+        @pl.when(r != end_core)
+        def _():
+            got(rows_out.at[pl.ds(0, fewer)], m_r)
     out = rows_out[...].T
     mixed_ref[...] = jnp.where(r == 0, out[:feat], out[feat:])
     with jax.named_scope("fin"):
@@ -342,9 +449,27 @@
         logits = jnp.where(lane == j, outs[j] + ob_ref[j], logits)
     scores_ref[...] = jax.nn.sigmoid(logits.T[:tasks, :])
     with jax.named_scope("end"):
-        sent(zrec.at[:, pl.ds(0, nt - 1)], z_s)
-        sent(rows_out.at[pl.ds(0, half)], m_s)
+        @pl.when(r == end_core)
+        def _():
+            sent(zrec.at[0], zl_s.at[0])
+            sent(zrec.at[1, pl.ds(0, nt - 1)], zl_s.at[1])
+            sent(rows_out.at[pl.ds(0, fewer)], m_s)
+
+        @pl.when(r != end_core)
+        def _():
+            sent(rows_out.at[pl.ds(0, half)], m_s)
         sent(frecv.at[pl.ds(0, nt - 1)], f_s)
+
+
+def emit_kernel(mixed_in, scores_in, mixed_out, scores_out, sem):
+    copies = [
+        pltpu.make_async_copy(mixed_in, mixed_out, sem.at[0]),
+        pltpu.make_async_copy(scores_in, scores_out, sem.at[1]),
+    ]
+    for copy in copies:
+        copy.start()
+    for copy in copies:
+        copy.wait()
 
 
 def stay_device(requests, expert_ids, gate_values, w_up, w_down, tower_in, tower_bias, tower_out,
@@ -379,9 +504,12 @@
         pltpu.VMEM((nt, nx, unit, wide), BF16), pltpu.VMEM((nt, nt, unit, wide), BF16),
         pltpu.VMEM((nt, unit, tasks * th), BF16), pltpu.VMEM((nt, unit, tasks * th), BF16),
         pltpu.VMEM((tok, wide), BF16),
+        pltpu.VMEM((nr, nx, unit, wide), BF16), pltpu.VMEM((nx, unit, wide), BF16),
+        pltpu.VMEM((nt, unit, wide), BF16),
         dma((8,)), dma, dma, dma, dma((C,)), dma, dma((C,)),
-        dma, dma((C, 2, 2)), dma, dma((C, 2)), dma((2,)), dma((C, 2, 3)),
-        dma, dma((nt,)), dma, dma((nt, nx - 1)), dma, dma((nt,)), dma, dma, dma, dma, dma, dma,
+        dma, dma((C, 2)), dma, dma((C, 2)), dma((2,)), dma((C, 2, 2)),
+        dma, dma((nt,)), dma, dma((nt,)), dma, dma((nt,)), dma, dma, dma, dma, dma, dma,
+        dma, dma((nx,)), dma((2,)), dma,
     ]
     mixed, scores = pl.pallas_call(
         functools.partial(stay_kernel, dims),
@@ -393,6 +521,14 @@
             has_side_effects=True, collective_id=0, vmem_limit_bytes=60 << 20),
         name="stay",
     )(requests.T, expert_ids.T, gate_values.T, w_up, w_down, tower_in, tower_bias, tower_out, out_bias)
+    mixed, scores = pl.pallas_call(
+        emit_kernel,
+        out_shape=(jax.ShapeDtypeStruct(mixed.shape, BF16), jax.ShapeDtypeStruct(scores.shape, F32)),
+        in_specs=[vmem, vmem],
+        out_specs=(hbm, hbm),
+        scratch_shapes=[dma((2,))],
+        name="emit",
+    )(pltpu.with_memory_space_constraint(mixed, pltpu.VMEM), pltpu.with_memory_space_constraint(scores, pltpu.VMEM))
     return mixed.T, scores
 
 

time: 55.8 us -> 53.8 us (0.964)
  local copies, waits for them, and re-layouts: 1.2 us -> 0 us
  Pallas kernels: 53.4 us -> 52.5 us
    pallas_call x1, Pallas kernels: 53.4 us -> 51.9 us  [stay_device(): pl.pallas_call(functools.partial(stay_kernel, dims), out_shape=(pltpu.VME...]
    unnamed x2 -> x0, local copies, waits for them, and re-layouts: 1.2 us -> none
    pallas_call x0 -> x1, Pallas kernels: none -> 0.64 us  [stay_device(): pl.pallas_call(emit_kernel, out_shape=(jax.ShapeDtypeStruct(mixed.shape,...]
where the time goes in v3:
time: 53.8 us; the launch traced here: 53.1 us
  Pallas kernels  52.5 us (98%)
  between operations  0.64 us (1%)
    pallas_call x1, Pallas kernels, stay_device(): pl.pallas_call(functools.partial(stay_kernel, dims), out_shape=(pltpu.VME...  51.9 us

profile of v3, /device:TPU:25, one launch (start us, length us, event | category | flops | bytes accessed | tf_op | source)
XLA Modules:
  0.0 53.1 jit_solution(7196192949889145024)
XLA Ops:
  0.6 51.9 %stay.1 = (bf16[192,128]{1,0:T(8,128)(2,1)S(1)}, f32[3,16]{1,0:T(4,128)S(1)}) custom-call(bf16[192,128]{1,0:T(8,128)(2,1)} %bitcast.4, s32[2,128]{1,0:T(2,128)} %bitcast.5, f32[2,128]{1,0:T(2,128)} %bitcast.6, bf16[4,384,768]{2,1,0:T(8,128)(2,1)} %up_hbm.1, bf16[4,384,768]{2,1,0:T(8,128)(2,1)} %down_hbm.1, bf16[192,768]{1,0:T(8,128)(2,1)} %tin_hbm.1, ...), custom_call_target="tpu_custom_call" | custom-call | tf_op jit(solution)/shard_map/stay/pallas_call | solution.py:514
  52.5 0.6 %emit.1 = (bf16[192,128]{1,0:T(8,128)(2,1)}, f32[3,16]{1,0:T(4,128)}) custom-call(bf16[192,128]{1,0:T(8,128)(2,1)S(1)} %get-tuple-element.6.mixed_in, f32[3,16]{1,0:T(4,128)S(1)} %get-tuple-element.7.scores_in), custom_call_target="tpu_custom_call" | custom-call | tf_op jit(solution)/shard_map/emit/pallas_call | solution.py:524

commit v4 on v3

--- a/solution.py
+++ b/solution.py
@@ -15,9 +15,9 @@
     dims, req_hbm, ids_hbm, gates_hbm, up_hbm, down_hbm, tin_hbm, bias_hbm, tout_hbm, ob_ref,
     mixed_ref, scores_ref,
     req_ref, ids_ref, gates_ref, bias_ref, tout_ref, up, down, tin, meta_ref, meta, rt, xs,
-    hp, r1, s2, r2, hid, mine, dsend0, drecv0, dsend, gat, zrec, fsend, frecv, rows_out, lrec, lsum, zl,
+    hp, r1, s2, r2, hid, mine, dsend0, drecv0, dsend, gat, zrec, fsend, frecv, rows_out, lrec, lsum, zl, ow, owt, pre_ref,
     lsem, me_s, me_r, x_s, x_r, q_s, q_r, s1_s, s1_r, s2_s, s2_r, h_s, h_r,
-    p_s, p_r, g_s, g_r, z_s, z_r, m_s, m_r, t_s, t_r, f_s, f_r, l_s, l_r, zl_s, zl_r,
+    p_s, p_r, g_s, g_r, z_s, z_r, m_s, m_r, t_s, t_r, f_s, f_r, l_s, l_r, zl_s, zl_r, o_s, o_r, w_s, w_r, v_s, v_r,
 ):
     nx, nt, nr, experts, tok, feat, hcols, tasks, th, unit, sizes = dims
     xe, t, r = lax.axis_index("expert"), lax.axis_index("tensor"), lax.axis_index("rep")
@@ -191,6 +191,32 @@
         got(hid.at[h, pl.ds(0, 2), picks(c)], h_r.at[c, h, 1])
 
     last = chunks - 1
+    own_t = nt - 1
+
+    def to_owner(source):
+        for q in range(own_t):
+            @pl.when(t != own_t)
+            def _():
+                send(source(q), ow.at[q, t], o_s, o_r, (xe, own_t, r))
+
+            @pl.when(t == own_t)
+            def _():
+                ow[q, own_t] = source(q)[...]
+
+    def tower_rows(c):
+        loads[2].wait()
+        got(own_rows(tin, 1 - r), t_r)
+
+        @pl.when(jnp.logical_and(r == end_core, t != own_t))
+        def _():
+            send(tin, owt.at[t], w_s, w_r, (xe, own_t, r))
+
+    def share_rows(c):
+        @pl.when(jnp.logical_and(r == end_core, t == own_t))
+        def _():
+            got(owt, w_r)
+            send(owt, owt, v_s, v_r, partner)
+
     end_core = (sum(sizes) - 1) % nr
     final_rows = pl.ds((sum(sizes) - 1) * unit, unit)
 
@@ -198,8 +224,10 @@
         return sum(sizes[:c]) % nr if sizes[c] == 1 else None
 
     def slot(c, core):
-        return (sum(sizes[:c]) + (sizes[c] - 1 if sizes[c] > 1 else 0)) // nr - (
-            core if sizes[c] > 1 else 0)
+        start = sum(sizes[:c])
+        if sizes[c] == 1 or start % nr == 0:
+            return start // nr
+        return start // nr + 1 - core
 
     def if_core(c, other, body, only=None):
         p = parity(c)
@@ -244,9 +272,9 @@
         if sizes[c] == 1:
             keep = give = total
         else:
-            odd, even = total[:, :unit], total[:, unit:]
-            keep = jnp.where(r == 0, even, odd)
-            give = jnp.where(r == 0, odd, even)
+            lead = sum(sizes[:c]) % nr
+            keep = jnp.where(r == lead, total[:, :unit], total[:, unit:])
+            give = jnp.where(r == lead, total[:, unit:], total[:, :unit])
 
         def store():
             mine[slot(c, r)] = keep
@@ -284,6 +312,7 @@
             def _():
                 got(lrec.at[:, q], l_r.at[q ^ xe])
                 last_sum(q)
+        to_owner(lambda q: lsum.at[q])
 
     def last_mixed():
         @pl.when(r == end_core)
@@ -298,15 +327,6 @@
             total = total + zl[src].astype(F32)
         value = total.astype(BF16)
         rows_out[final_rows, :] = value
-
-        @pl.when(r == end_core)
-        def _():
-            s = nt - 1
-            fsend[s] = jnp.dot(value, tin[...], preferred_element_type=F32).astype(BF16)
-
-            @pl.when(t != s)
-            def _():
-                send(fsend.at[s], frecv.at[t], f_s, f_r, (xe, s, r))
 
     def pair_chunk(c, only=None):
         if c == last:
@@ -339,6 +359,8 @@
                 @pl.when(q != t)
                 def _():
                     send(gat.at[s, q], zrec.at[s, t], z_s, z_r.at[s], (xe, q, r))
+            if c == last - 1:
+                to_owner(lambda q: gat.at[s, q])
         if_core(c, False, body, only)
 
     def mixed_chunk(c, only=None):
@@ -355,6 +377,8 @@
             at = pl.ds(pl.multiple_of((s * nr + r) * unit, unit), unit)
             rows_out[at, :] = value
             send(rows_out.at[at], rows_out.at[at], m_s, m_r, partner)
+            if c == last - 1:
+                return
             fsend[s] = jnp.dot(value, tin[...], preferred_element_type=F32).astype(BF16)
 
             @pl.when(t != s)
@@ -396,7 +420,7 @@
     stages = {
         "fw": forward, "rb": reduce_second, "ra": reduce_first, "up": up_chunk, "co": collect,
         "dn": down_chunk, "pr": pair_chunk, "ps": pass_chunk, "mx": mixed_chunk, "drain": drain,
-        "pe": last_own,
+        "pe": last_own, "tw": tower_rows, "tf": share_rows,
     }
     for core in range(nr):
         for name in ("pr", "ps", "mx"):
@@ -405,17 +429,21 @@
     for i in range(chunks + 4):
         order += [("up", i), ("ra", i - 1), ("rb", i - 2), ("fw", i - 3), ("co", i - 4), ("dn", i - 4)]
         if i < chunks + 3:
-            order += [("pr0", i - 4), ("pr1", i - 5), ("ps0", i - 5), ("ps1", i - 6), ("mx0", i - 6), ("mx1", i - 7)]
+            order += [("pr0", i - 4), ("pr1", i - 5)]
+            if i < chunks + 2:
+                order += [("ps0", i - 5)]
+            order += [("ps1", i - 6), ("mx0", i - 7), ("mx1", i - 7)]
     n = last
-    order += [("pr1", n - 1), ("ps0", n - 1), ("ps1", n - 2), ("mx0", n - 2), ("mx1", n - 3),
+    order += [("pr1", n - 1), ("ps0", n - 2), ("ps1", n - 2), ("mx0", n - 3), ("ps0", n - 1), ("mx0", n - 2), ("mx1", n - 3),
               ("ps1", n - 1), ("pe", n), ("mx1", n - 2), ("ps", n), ("mx0", n - 1), ("mx1", n - 1), ("drain", n), ("mx", n)]
+    order.insert(order.index(("up", 2)) + 1, ("tw", last))
+    order.insert(order.index(("dn", last)) + 1, ("tf", last))
     for name, c in order:
         if not 0 <= c < chunks or (c == last and name[-1].isdigit()):
             continue
         if name == "dn" and c == 0:
-            for load in loads[1:]:
+            for load in loads[1:2] + loads[3:]:
                 load.wait()
-            got(own_rows(tin, 1 - r), t_r)
         with jax.named_scope(f"{name}_{c}"):
             if name in ("fw", "rb", "ra", "co"):
                 for h in range(2):
@@ -435,10 +463,30 @@
     out = rows_out[...].T
     mixed_ref[...] = jnp.where(r == 0, out[:feat], out[feat:])
     with jax.named_scope("fin"):
-        got(frecv.at[pl.ds(0, nt - 1)], f_r)
-        pre = fsend[t].astype(F32)
-        for d in range(1, nt):
-            pre = pre + frecv[t ^ d].astype(F32)
+        @pl.when(t == own_t)
+        def _():
+            at = pl.ds(pl.multiple_of((own_t * nr + r) * unit, unit), unit)
+            got(ow.at[:, pl.ds(0, nt - 1)], o_r)
+
+            @pl.when(r != end_core)
+            def _():
+                got(owt, v_r)
+            pre = jnp.dot(rows_out[at, :], tin[...], preferred_element_type=F32)
+            for q in range(own_t):
+                total = ow[q, 0].astype(F32)
+                for src in range(1, nt):
+                    total = total + ow[q, src].astype(F32)
+                pre = pre + jnp.dot(total.astype(BF16), owt[q], preferred_element_type=F32)
+            pre_ref[...] = pre
+
+        @pl.when(t != own_t)
+        def _():
+            got(frecv.at[pl.ds(0, nt - 1)], f_r)
+            pre = fsend[t].astype(F32)
+            for d in range(1, nt):
+                pre = pre + frecv[t ^ d].astype(F32)
+            pre_ref[...] = pre
+        pre = pre_ref[...]
     active = jnp.maximum(pre + bias_ref[...].reshape(1, tasks * th), 0.0)
     outs = []
     for j in range(tasks):
@@ -458,7 +506,22 @@
         @pl.when(r != end_core)
         def _():
             sent(rows_out.at[pl.ds(0, half)], m_s)
-        sent(frecv.at[pl.ds(0, nt - 1)], f_s)
+        @pl.when(t == own_t)
+        def _():
+            sent(frecv.at[pl.ds(0, nt - 1)], f_s)
+
+        @pl.when(t != own_t)
+        def _():
+            sent(frecv.at[pl.ds(0, nt - 2)], f_s)
+            sent(ow.at[0, pl.ds(0, nt - 1)], o_s)
+
+        @pl.when(jnp.logical_and(r == end_core, t == own_t))
+        def _():
+            sent(owt, v_s)
+
+        @pl.when(jnp.logical_and(r == end_core, t != own_t))
+        def _():
+            sent(tin, w_s)
 
 
 def emit_kernel(mixed_in, scores_in, mixed_out, scores_out, sem):
@@ -480,7 +543,7 @@
     tasks, th = tower_out.shape
     hcols = hid_cols // 2
     unit = tok // (nt * nr)
-    sizes = (1,) + (nr,) * (nt - 1) + (1,)
+    sizes = (nr,) * (nt - 1) + (1,) * nr
     C = len(sizes)
     dims = (nx, nt, nr, experts, tok, feat, hcols, tasks, th, unit, sizes)
     vmem = pl.BlockSpec(memory_space=pltpu.VMEM)
@@ -506,10 +569,13 @@
         pltpu.VMEM((tok, wide), BF16),
         pltpu.VMEM((nr, nx, unit, wide), BF16), pltpu.VMEM((nx, unit, wide), BF16),
         pltpu.VMEM((nt, unit, wide), BF16),
+        pltpu.VMEM((nt - 1, nt, unit, wide), BF16),
+        pltpu.VMEM((nt - 1, wide, tower_in.shape[1]), BF16),
+        pltpu.VMEM((unit, tower_in.shape[1]), F32),
         dma((8,)), dma, dma, dma, dma((C,)), dma, dma((C,)),
         dma, dma((C, 2)), dma, dma((C, 2)), dma((2,)), dma((C, 2, 2)),
         dma, dma((nt,)), dma, dma((nt,)), dma, dma((nt,)), dma, dma, dma, dma, dma, dma,
-        dma, dma((nx,)), dma((2,)), dma,
+        dma, dma((nx,)), dma((2,)), dma, dma, dma, dma, dma, dma, dma,
     ]
     mixed, scores = pl.pallas_call(
         functools.partial(stay_kernel, dims),

time: 53.8 us -> 52.5 us (0.976)
  Pallas kernels: 52.5 us -> 51.7 us
    pallas_call x1, Pallas kernels: 51.9 us -> 51.1 us  [stay_device(): pl.pallas_call(functools.partial(stay_kernel, dims), out_shape=(pltpu.VME...]
where the time goes in v4:
time: 52.5 us; the launch traced here: 52.3 us
  Pallas kernels  51.7 us (98%)
  between operations  0.64 us (1%)
    pallas_call x1, Pallas kernels, stay_device(): pl.pallas_call(functools.partial(stay_kernel, dims), out_shape=(pltpu.VME...  51.1 us

profile of v4, /device:TPU:25, one launch (start us, length us, event | category | flops | bytes accessed | tf_op | source)
XLA Modules:
  0.0 52.3 jit_solution(8134144398557371304)
XLA Ops:
  0.6 51.1 %stay.1 = (bf16[192,128]{1,0:T(8,128)(2,1)S(1)}, f32[3,16]{1,0:T(4,128)S(1)}) custom-call(bf16[192,128]{1,0:T(8,128)(2,1)} %bitcast.4, s32[2,128]{1,0:T(2,128)} %bitcast.5, f32[2,128]{1,0:T(2,128)} %bitcast.6, bf16[4,384,768]{2,1,0:T(8,128)(2,1)} %up_hbm.1, bf16[4,384,768]{2,1,0:T(8,128)(2,1)} %down_hbm.1, bf16[192,768]{1,0:T(8,128)(2,1)} %tin_hbm.1, ...), custom_call_target="tpu_custom_call" | custom-call | tf_op jit(solution)/shard_map/stay/pallas_call | solution.py:580
  51.7 0.6 %emit.1 = (bf16[192,128]{1,0:T(8,128)(2,1)}, f32[3,16]{1,0:T(4,128)}) custom-call(bf16[192,128]{1,0:T(8,128)(2,1)S(1)} %get-tuple-element.6.mixed_in, f32[3,16]{1,0:T(4,128)S(1)} %get-tuple-element.7.scores_in), custom_call_target="tpu_custom_call" | custom-call | tf_op jit(solution)/shard_map/emit/pallas_call | solution.py:590

commit v5 on v4

--- a/solution.py
+++ b/solution.py
@@ -23,6 +23,12 @@
     xe, t, r = lax.axis_index("expert"), lax.axis_index("tensor"), lax.axis_index("rep")
     chunks = len(sizes)
     offs = [sum(sizes[:c]) * unit for c in range(chunks)]
+    low = feat // 128 * 128
+    rem = feat - low
+    starts = [sum(sizes[:c]) for c in range(chunks)]
+    extra = [unit if n > 1 or start % nr == 0 else 0 for n, start in zip(sizes, starts)]
+    plan = [n * unit + e for n, e in zip(sizes, extra)]
+    base = [sum(plan[:c]) for c in range(chunks)]
     subs = [n * unit for n in sizes]
 
     def remote(src, dst, ssem, rsem, dev):
@@ -71,33 +77,45 @@
     for d in range(1, nx):
         for k in range(nr):
             greet((xe ^ d, t, k))
-    for b in range(nx):
-        @pl.when(jnp.logical_not(jnp.logical_and(here, xe == b)))
-        def _():
-            greet((b, xe, r))
+    hub = nr - 1
+
+    @pl.when(r == hub)
+    def _():
+        for b in range(nx):
+            for k in range(hub):
+                greet((b, xe, k))
+
+            @pl.when(jnp.logical_not(jnp.logical_and(here, xe == b)))
+            def _():
+                greet((b, xe, hub))
     for load in first[1:] + loads:
         load.start()
     first[0].wait()
-    rt[...] = req_ref[...].T
+    full = req_ref[...].T
+    for c in range(chunks):
+        rt[base[c]:base[c] + subs[c], :] = full[offs[c]:offs[c] + subs[c], :low]
+        if extra[c]:
+            rt[base[c] + subs[c]:base[c] + plan[c], :] = jnp.concatenate(
+                [full[offs[c] + k * unit:offs[c] + (k + 1) * unit, low:] for k in range(nr)], axis=1)
     greeted = (nt * nr - 1) + (nx - 1) * nr + nt
 
     with jax.named_scope("barr"):
-        @pl.when(here)
+        @pl.when(jnp.logical_and(here, r == hub))
         def _():
             pl.semaphore_wait(barrier, greeted - 1)
 
-        @pl.when(away)
+        @pl.when(jnp.logical_or(away, r != hub))
         def _():
             pl.semaphore_wait(barrier, greeted)
 
     def span(c):
-        return pl.ds(offs[c], subs[c])
+        return pl.ds(base[c], plan[c])
 
     for c in range(chunks):
         for tt in reversed(range(nt)):
-            @pl.when(jnp.logical_not(jnp.logical_and(here, t == tt)))
-            def _():
-                send(rt.at[span(c)], xs.at[r, xe, span(c)], x_s, x_r.at[c], (t, tt, r))
+            @pl.when(jnp.logical_not(jnp.logical_and(jnp.logical_and(here, t == tt), r == hub)))
+            def _():
+                send(rt.at[span(c)], xs.at[r, xe, span(c)], x_s, x_r.at[r, c], (t, tt, hub))
         if c == 0:
             for load in first[1:]:
                 load.wait()
@@ -108,19 +126,24 @@
     send(tin_hbm, own_rows(tin, r), t_s, t_r, partner)
     meta[xe] = meta_ref[...]
 
-    @pl.when(here)
+    @pl.when(jnp.logical_and(here, r == hub))
     def _():
-        xs[r, xe] = rt[...]
+        xs[hub, xe] = rt[...]
 
     def take(c):
-        @pl.when(here)
-        def _():
-            got(xs.at[r, pl.ds(0, nx - 1), span(c)], x_r.at[c])
-
-        @pl.when(away)
-        def _():
-            got(xs.at[r, :, span(c)], x_r.at[c])
-        send(xs.at[r, :, span(c)], xs.at[r, :, span(c)], q_s, q_r.at[c], partner)
+        @pl.when(r == hub)
+        def _():
+            for k in range(hub):
+                got(xs.at[k, :, span(c)], x_r.at[k, c])
+
+            @pl.when(here)
+            def _():
+                got(xs.at[hub, pl.ds(0, nx - 1), span(c)], x_r.at[hub, c])
+
+            @pl.when(away)
+            def _():
+                got(xs.at[hub, :, span(c)], x_r.at[hub, c])
+            send(xs.at[:, :, span(c)], xs.at[:, :, span(c)], q_s, q_r.at[c], partner)
 
     with jax.named_scope("take0"):
         take(0)
@@ -141,10 +164,24 @@
 
     def up_chunk(c):
         sub = subs[c]
-        got(xs.at[1 - r, :, span(c)], q_r.at[c])
+        @pl.when(r != hub)
+        def _():
+            got(xs.at[:, :, span(c)], q_r.at[c])
         if c == 0:
             loads[0].wait()
-        rows = [xs[k, :, offs[c]:offs[c] + sub, :].reshape(nx * sub, feat) for k in range(nr)]
+        from_chunk = c if extra[c] else c - 1
+        tail_at = base[from_chunk] + subs[from_chunk]
+        first_unit = starts[c] % nr
+        rows = []
+        for k in range(nr):
+            parts = []
+            for b in range(nx):
+                main = xs[k, b, base[c]:base[c] + sub, :]
+                side = xs[k, b, tail_at:tail_at + unit, :]
+                side = [side[:, u * rem:(u + 1) * rem] for u in range(first_unit, first_unit + sizes[c])]
+                side = side[0] if len(side) == 1 else jnp.concatenate(side, axis=0)
+                parts.append(jnp.concatenate([main, side], axis=1))
+            rows.append(jnp.concatenate(parts, axis=0))
         ids = (column(c, 0), column(c, 1))
         for h in range(2):
             picked = [jnp.zeros((nx * sub, hcols), F32)] * 2
@@ -159,36 +196,40 @@
                 hp[h, :, picks(c, k), :] = picked[k].astype(BF16).reshape(nx, sub, hcols)
             fa, fb = near[h], near[1 - h]
             for i, q, sem in ((0, xe ^ fa ^ fb, s1_r), (1, xe ^ fa, s2_r)):
-                send(hp.at[h, q, picks(c)], r1.at[h, i, picks(c)], s1_s, sem.at[c, h],
+                send(hp.at[h, q, picks(c)], r1.at[h, i, picks(c)], s1_s, sem.at[c],
                      (xe ^ fa, t, r))
         if c + 1 < chunks:
             take(c + 1)
 
     def reduce_first(c, h):
         fa, fb = near[h], near[1 - h]
-        got(r1.at[h, 0, picks(c)], s1_r.at[c, h])
+        if h == 0:
+            got(r1.at[:, 0, picks(c)], s1_r.at[c])
         s2[h, picks(c)] = (hp[h, xe ^ fb, picks(c)].astype(F32)
                            + r1[h, 0, picks(c)].astype(F32)).astype(BF16)
-        send(s2.at[h, picks(c)], r2.at[h, picks(c)], s2_s, s2_r.at[c, h], (xe ^ fb, t, r))
+        send(s2.at[h, picks(c)], r2.at[h, picks(c)], s2_s, s2_r.at[c], (xe ^ fb, t, r))
 
     def reduce_second(c, h):
         fa, fb = near[h], near[1 - h]
-        got(r1.at[h, :, picks(c)], s2_r.at[c, h])
+        if h == 0:
+            got(r1.at[:, :, picks(c)], s2_r.at[c])
         total = (hp[h, xe, picks(c)].astype(F32) + r1[h, 1, picks(c)].astype(F32)
                  + r2[h, picks(c)].astype(F32))
         hid[h, xe, picks(c)] = jnp.maximum(total, 0.0).astype(BF16)
         mine_ref = hid.at[h, xe, picks(c)]
-        send(mine_ref, mine_ref, h_s.at[0], h_r.at[c, h, 0], (xe ^ fb, t, r))
-        send(mine_ref, mine_ref, h_s.at[0], h_r.at[c, h, 1], (xe ^ fa, t, r))
+        send(mine_ref, mine_ref, h_s.at[0], h_r.at[c, 0], (xe ^ fb, t, r))
+        send(mine_ref, mine_ref, h_s.at[0], h_r.at[c, 1], (xe ^ fa, t, r))
 
     def forward(c, h):
         fa, fb = near[h], near[1 - h]
         ref = hid.at[h, xe ^ fb, picks(c)]
-        got(ref, h_r.at[c, h, 0])
-        send(ref, ref, h_s.at[1], h_r.at[c, h, 1], (xe ^ fa, t, r))
+        if h == 0:
+            got(hid.at[:, 0, picks(c)], h_r.at[c, 0])
+        send(ref, ref, h_s.at[1], h_r.at[c, 1], (xe ^ fa, t, r))
 
     def collect(c, h):
-        got(hid.at[h, pl.ds(0, 2), picks(c)], h_r.at[c, h, 1])
+        if h == 0:
+            got(hid.at[:, pl.ds(0, 2), picks(c)], h_r.at[c, 1])
 
     last = chunks - 1
     own_t = nt - 1
@@ -393,7 +434,11 @@
         sent(r2, h_s.at[1])
         sent(meta.at[pl.ds(0, nx - 1)], me_s)
         sent(own_rows(tin, r), t_s)
-        sent(xs.at[r], q_s)
+
+        @pl.when(r == hub)
+        def _():
+            sent(xs, q_s)
+
 
         @pl.when(r == end_core)
         def _():
@@ -409,11 +454,11 @@
             sent(gat.at[:, pl.ds(0, nx - 1)], g_s)
             sent(zrec.at[:, pl.ds(0, nt - 1)], z_s)
 
-        @pl.when(here)
+        @pl.when(jnp.logical_and(here, r == hub))
         def _():
             sent(xs.at[r, pl.ds(0, nx - 1)], x_s)
 
-        @pl.when(away)
+        @pl.when(jnp.logical_or(away, r != hub))
         def _():
             sent(xs.at[r], x_s)
 
@@ -426,14 +471,14 @@
         for name in ("pr", "ps", "mx"):
             stages[f"{name}{core}"] = functools.partial(stages[name], only=core)
     order = []
-    for i in range(chunks + 4):
-        order += [("up", i), ("ra", i - 1), ("rb", i - 2), ("fw", i - 3), ("co", i - 4), ("dn", i - 4)]
-        if i < chunks + 3:
-            order += [("pr0", i - 4), ("pr1", i - 5)]
-            if i < chunks + 2:
-                order += [("ps0", i - 5)]
-            order += [("ps1", i - 6), ("mx0", i - 7), ("mx1", i - 7)]
     n = last
+    for i in range(n):
+        order += [("up", i), ("ra", i - 1), ("rb", i - 2), ("fw", i - 3)]
+    order += [("up", n), ("ra", n - 1), ("rb", n - 2), ("fw", n - 3), ("ra", n), ("co", n - 4), ("dn", n - 4), ("pr0", n - 4),
+              ("rb", n - 1), ("fw", n - 2), ("rb", n), ("co", n - 3), ("dn", n - 3), ("pr0", n - 3), ("pr1", n - 4), ("ps0", n - 4),
+              ("fw", n - 1), ("fw", n), ("co", n - 2), ("dn", n - 2), ("pr0", n - 2), ("pr1", n - 3), ("ps0", n - 3), ("ps1", n - 4),
+              ("co", n - 1), ("dn", n - 1), ("pr0", n - 1), ("pr1", n - 2), ("ps1", n - 3), ("mx0", n - 4), ("mx1", n - 4),
+              ("co", n), ("dn", n)]
     order += [("pr1", n - 1), ("ps0", n - 2), ("ps1", n - 2), ("mx0", n - 3), ("ps0", n - 1), ("mx0", n - 2), ("mx1", n - 3),
               ("ps1", n - 1), ("pe", n), ("mx1", n - 2), ("ps", n), ("mx0", n - 1), ("mx1", n - 1), ("drain", n), ("mx", n)]
     order.insert(order.index(("up", 2)) + 1, ("tw", last))
@@ -557,7 +602,7 @@
         pltpu.VMEM(w_up.shape, BF16), pltpu.VMEM(w_down.shape, BF16),
         pltpu.VMEM((wide, tower_in.shape[1]), BF16),
         pltpu.VMEM((8, tok), F32), pltpu.VMEM((nx, 8, tok), F32),
-        pltpu.VMEM((tok, feat), BF16), pltpu.VMEM((nr, nx, tok, feat), BF16),
+        pltpu.VMEM((tok * feat // 128, 128), BF16), pltpu.VMEM((nr, nx, tok * feat // 128, 128), BF16),
         pltpu.VMEM((2, nx, 2 * tok, hcols), BF16),
         pltpu.VMEM((2, 2, 2 * tok, hcols), BF16),
         pltpu.VMEM((2, 2 * tok, hcols), BF16), pltpu.VMEM((2, 2 * tok, hcols), BF16),
@@ -572,8 +617,8 @@
         pltpu.VMEM((nt - 1, nt, unit, wide), BF16),
         pltpu.VMEM((nt - 1, wide, tower_in.shape[1]), BF16),
         pltpu.VMEM((unit, tower_in.shape[1]), F32),
-        dma((8,)), dma, dma, dma, dma((C,)), dma, dma((C,)),
-        dma, dma((C, 2)), dma, dma((C, 2)), dma((2,)), dma((C, 2, 2)),
+        dma((8,)), dma, dma, dma, dma((nr, C)), dma, dma((C,)),
+        dma, dma((C,)), dma, dma((C,)), dma((2,)), dma((C, 2)),
         dma, dma((nt,)), dma, dma((nt,)), dma, dma((nt,)), dma, dma, dma, dma, dma, dma,
         dma, dma((nx,)), dma((2,)), dma, dma, dma, dma, dma, dma, dma,
     ]

time: 52.5 us -> 51.8 us (0.987)
  Pallas kernels: 51.7 us -> 50.9 us
    pallas_call x1, Pallas kernels: 51.1 us -> 50.3 us  [stay_device(): pl.pallas_call(functools.partial(stay_kernel, dims), out_shape=(pltpu.VME...]
where the time goes in v5:
time: 51.8 us; the launch traced here: 51.6 us
  Pallas kernels  50.9 us (98%)
  between operations  0.64 us (1%)
    pallas_call x1, Pallas kernels, stay_device(): pl.pallas_call(functools.partial(stay_kernel, dims), out_shape=(pltpu.VME...  50.3 us

profile of v5, /device:TPU:25, one launch (start us, length us, event | category | flops | bytes accessed | tf_op | source)
XLA Modules:
  0.0 51.6 jit_solution(10928372175412536030)
XLA Ops:
  0.6 50.3 %stay.1 = (bf16[192,128]{1,0:T(8,128)(2,1)S(1)}, f32[3,16]{1,0:T(4,128)S(1)}) custom-call(bf16[192,128]{1,0:T(8,128)(2,1)} %bitcast.4, s32[2,128]{1,0:T(2,128)} %bitcast.5, f32[2,128]{1,0:T(2,128)} %bitcast.6, bf16[4,384,768]{2,1,0:T(8,128)(2,1)} %up_hbm.1, bf16[4,384,768]{2,1,0:T(8,128)(2,1)} %down_hbm.1, bf16[192,768]{1,0:T(8,128)(2,1)} %tin_hbm.1, ...), custom_call_target="tpu_custom_call" | custom-call | tf_op jit(solution)/shard_map/stay/pallas_call | solution.py:625
  50.9 0.6 %emit.1 = (bf16[192,128]{1,0:T(8,128)(2,1)}, f32[3,16]{1,0:T(4,128)}) custom-call(bf16[192,128]{1,0:T(8,128)(2,1)S(1)} %get-tuple-element.6.mixed_in, f32[3,16]{1,0:T(4,128)S(1)} %get-tuple-element.7.scores_in), custom_call_target="tpu_custom_call" | custom-call | tf_op jit(solution)/shard_map/emit/pallas_call | solution.py:635

commit v6 on v5

--- a/solution.py
+++ b/solution.py
@@ -299,16 +299,16 @@
         total = total.reshape(nx, sub, nr * feat)
         if c == last:
             dsend0[c] = total.astype(BF16)
+
+            @pl.when(r != end_core)
+            def _():
+                send(dsend0.at[c, xe], lrec.at[r, xe], l_s, l_r.at[0], partner)
             for d in (3, 1, 2):
                 send(dsend0.at[c, xe ^ d], lrec.at[r, xe], l_s, l_r.at[d], (xe ^ d, t, end_core))
 
             @pl.when(r == end_core)
             def _():
                 lrec[r, xe] = dsend0[c, xe]
-
-            @pl.when(r != end_core)
-            def _():
-                send(dsend0.at[c, xe], lrec.at[r, xe], l_s, l_r.at[0], partner)
             return
         if sizes[c] == 1:
             keep = give = total
@@ -479,8 +479,9 @@
               ("fw", n - 1), ("fw", n), ("co", n - 2), ("dn", n - 2), ("pr0", n - 2), ("pr1", n - 3), ("ps0", n - 3), ("ps1", n - 4),
               ("co", n - 1), ("dn", n - 1), ("pr0", n - 1), ("pr1", n - 2), ("ps1", n - 3), ("mx0", n - 4), ("mx1", n - 4),
               ("co", n), ("dn", n)]
-    order += [("pr1", n - 1), ("ps0", n - 2), ("ps1", n - 2), ("mx0", n - 3), ("ps0", n - 1), ("mx0", n - 2), ("mx1", n - 3),
-              ("ps1", n - 1), ("pe", n), ("mx1", n - 2), ("ps", n), ("mx0", n - 1), ("mx1", n - 1), ("drain", n), ("mx", n)]
+    order += [("pr1", n - 1), ("ps0", n - 2), ("mx0", n - 3), ("ps0", n - 1), ("mx0", n - 2),
+              ("ps1", n - 2), ("pe", n), ("mx1", n - 3), ("ps1", n - 1), ("ps", n),
+              ("mx1", n - 2), ("mx0", n - 1), ("mx1", n - 1), ("drain", n), ("mx", n)]
     order.insert(order.index(("up", 2)) + 1, ("tw", last))
     order.insert(order.index(("dn", last)) + 1, ("tf", last))
     for name, c in order:

time: 51.8 us -> 51.8 us (level)
  no operation moved by 1% of the time
where the time goes in v6:
time: 51.8 us; the launch traced here: 51.3 us
  Pallas kernels  50.6 us (98%)
  between operations  0.64 us (1%)
    pallas_call x1, Pallas kernels, stay_device(): pl.pallas_call(functools.partial(stay_kernel, dims), out_shape=(pltpu.VME...  50 us

profile of v6, /device:TPU:25, one launch (start us, length us, event | category | flops | bytes accessed | tf_op | source)
XLA Modules:
  0.0 51.3 jit_solution(7165661363638691808)
XLA Ops:
  0.6 50.0 %stay.1 = (bf16[192,128]{1,0:T(8,128)(2,1)S(1)}, f32[3,16]{1,0:T(4,128)S(1)}) custom-call(bf16[192,128]{1,0:T(8,128)(2,1)} %bitcast.4, s32[2,128]{1,0:T(2,128)} %bitcast.5, f32[2,128]{1,0:T(2,128)} %bitcast.6, bf16[4,384,768]{2,1,0:T(8,128)(2,1)} %up_hbm.1, bf16[4,384,768]{2,1,0:T(8,128)(2,1)} %down_hbm.1, bf16[192,768]{1,0:T(8,128)(2,1)} %tin_hbm.1, ...), custom_call_target="tpu_custom_call" | custom-call | tf_op jit(solution)/shard_map/stay/pallas_call | solution.py:626
  50.6 0.6 %emit.1 = (bf16[192,128]{1,0:T(8,128)(2,1)}, f32[3,16]{1,0:T(4,128)}) custom-call(bf16[192,128]{1,0:T(8,128)(2,1)S(1)} %get-tuple-element.6.mixed_in, f32[3,16]{1,0:T(4,128)S(1)} %get-tuple-element.7.scores_in), custom_call_target="tpu_custom_call" | custom-call | tf_op jit(solution)/shard_map/emit/pallas_call | solution.py:636

commit v7 on v5

--- a/solution.py
+++ b/solution.py
@@ -70,6 +70,17 @@
     def greet(dev):
         pl.semaphore_signal(barrier, inc=1, device_id=dev, device_id_type=MESH)
 
+    hub = nr - 1
+
+    @pl.when(r == hub)
+    def _():
+        for b in range(nx):
+            for k in range(hub):
+                greet((b, xe, k))
+
+            @pl.when(jnp.logical_not(jnp.logical_and(here, xe == b)))
+            def _():
+                greet((b, xe, hub))
     me = t * nr + r
     for d in reversed(range(1, nt * nr)):
         other = me ^ d
@@ -77,17 +88,6 @@
     for d in range(1, nx):
         for k in range(nr):
             greet((xe ^ d, t, k))
-    hub = nr - 1
-
-    @pl.when(r == hub)
-    def _():
-        for b in range(nx):
-            for k in range(hub):
-                greet((b, xe, k))
-
-            @pl.when(jnp.logical_not(jnp.logical_and(here, xe == b)))
-            def _():
-                greet((b, xe, hub))
     for load in first[1:] + loads:
         load.start()
     first[0].wait()

time: 51.8 us -> 51.9 us (level)
  no operation moved by 1% of the time
where the time goes in v7:
time: 51.9 us; the launch traced here: 51.5 us
  Pallas kernels  50.9 us (98%)
  between operations  0.64 us (1%)
    pallas_call x1, Pallas kernels, stay_device(): pl.pallas_call(functools.partial(stay_kernel, dims), out_shape=(pltpu.VME...  50.2 us

profile of v7, /device:TPU:25, one launch (start us, length us, event | category | flops | bytes accessed | tf_op | source)
XLA Modules:
  0.0 51.5 jit_solution(12068476537790737476)
XLA Ops:
  0.6 50.2 %stay.1 = (bf16[192,128]{1,0:T(8,128)(2,1)S(1)}, f32[3,16]{1,0:T(4,128)S(1)}) custom-call(bf16[192,128]{1,0:T(8,128)(2,1)} %bitcast.4, s32[2,128]{1,0:T(2,128)} %bitcast.5, f32[2,128]{1,0:T(2,128)} %bitcast.6, bf16[4,384,768]{2,1,0:T(8,128)(2,1)} %up_hbm.1, bf16[4,384,768]{2,1,0:T(8,128)(2,1)} %down_hbm.1, bf16[192,768]{1,0:T(8,128)(2,1)} %tin_hbm.1, ...), custom_call_target="tpu_custom_call" | custom-call | tf_op jit(solution)/shard_map/stay/pallas_call | solution.py:625
  50.9 0.6 %emit.1 = (bf16[192,128]{1,0:T(8,128)(2,1)}, f32[3,16]{1,0:T(4,128)}) custom-call(bf16[192,128]{1,0:T(8,128)(2,1)S(1)} %get-tuple-element.6.mixed_in, f32[3,16]{1,0:T(4,128)S(1)} %get-tuple-element.7.scores_in), custom_call_target="tpu_custom_call" | custom-call | tf_op jit(solution)/shard_map/emit/pallas_call | solution.py:635
